TPU v7x, 256 devices: a whole 4x4x8 slice. The times are simulated.
256 devices in a mesh: batch: 16 (over y, x), cols: 16 (over z, core).
Axes of the slice: x: 4, y: 4, z: 8, core: 2. Of those that a mesh axis runs over, the one named last changes fastest.
Arguments:
- grad_query: float32 [16, 2048, 2048], P('batch', None, 'cols'), may hold values from -0.875 to 0.875
- grad_key: float32 [16, 2048, 2048], P('batch', None, 'cols'), may hold values from -0.875 to 0.875
- grad_value: float32 [16, 2048, 2048], P('batch', None, 'cols'), may hold values from -0.875 to 0.875
- grad_mixed: float32 [16, 2048, 2048], P('batch', 'cols'), may hold values from -0.875 to 0.875
- grad_norm: float32 [16, 2048], P('batch'), may hold values from -8 to 8
- grad_bias: float32 [16, 2048], P('batch'), may hold values from -8 to 8
- weight_query: float32 [2048, 2048], P('batch', 'cols'), may hold values from -0.1875 to 0.1875
- weight_key: float32 [2048, 2048], P('batch', 'cols'), may hold values from -0.1875 to 0.1875
- weight_value: float32 [2048, 2048], P('batch', 'cols'), may hold values from -0.1875 to 0.1875
- weight_mixed: float32 [2048, 2048], P('cols', 'batch'), may hold values from -0.1875 to 0.1875
- weight_norm: float32 [2048], P('batch'), may hold values from 0.25 to 1.75
- weight_bias: float32 [2048], P('batch'), may hold values from -3 to 3
Outputs:
- copy_query: bfloat16 [2048, 2048], P(None, 'cols')
- copy_key: bfloat16 [2048, 2048], P(None, 'cols')
- copy_value: bfloat16 [2048, 2048], P(None, 'cols')
- copy_mixed: bfloat16 [2048, 2048], P('cols')
- copy_norm: bfloat16 [2048], replicated
- copy_bias: bfloat16 [2048], replicated
- new_query: float32 [2048, 2048], P('batch', 'cols')
- new_key: float32 [2048, 2048], P('batch', 'cols')
- new_value: float32 [2048, 2048], P('batch', 'cols')
- new_mixed: float32 [2048, 2048], P('cols', 'batch')
- new_norm: float32 [2048], P('batch')
- new_bias: float32 [2048], P('batch')
All inputs are finite; a program needn't handle non-finite values.
Results may differ from a plain program's by a relative error of at most 0.0004.
Values may be sent and summed in bfloat16 or wider, within the bound.
A program may use at most 64 MiB of HBM per device.

v0:
```python
import jax
import jax.numpy as jnp
from jax import lax
from jax.sharding import PartitionSpec as P

learn_rate = 0.4


def in_blocks(shard, dim, size):
    dims = shard.shape
    blocks = shard.reshape(*dims[:dim], size, dims[dim] // size, *dims[dim + 1 :])
    return jnp.moveaxis(blocks, dim, 0)


def sum_packed(arrays, axis, dims):
    size = lax.axis_size(axis)
    blocks = [in_blocks(a, dim, size) for a, dim in zip(arrays, dims)]
    lines = jnp.concatenate([b.reshape(size, -1) for b in blocks], axis=1)
    rows = max(16, -(-lines.shape[1] // 1024) * 8)
    lines = jnp.pad(lines, ((0, 0), (0, rows * 128 - lines.shape[1]))).reshape(-1, 128)
    flat, at, gathered = (lax.psum_scatter(lines, axis, tiled=True).reshape(-1), 0, [])
    for b in blocks:
        part = b[0]
        gathered.append(flat[at : at + part.size].reshape(part.shape))
        at += part.size
    return tuple(gathered)


def from_everyone(shard, axis):
    copies = jnp.broadcast_to(shard, (lax.axis_size(axis), *shard.shape))
    return lax.all_to_all(copies, axis, split_axis=0, concat_axis=0, tiled=True)


def taken_together(shard, axis):
    return from_everyone(shard, axis).sum(axis=0)


def in_one(arrays, axis):
    ends = [0]
    for a in arrays:
        ends.append(ends[-1] + a.size)
    subtotal = taken_together(jnp.concatenate([a.ravel() for a in arrays]), axis)
    return tuple((subtotal[b:e].reshape(a.shape) for a, b, e in zip(arrays, ends, ends[1:])))


def gather_turned(arrays, axis, dims):
    turned = [jnp.moveaxis(a, dim, 0) for a, dim in zip(arrays, dims)]
    both = jnp.concatenate([t.reshape(len(t), -1) for t in turned], axis=1)
    whole, at, gathered = (lax.all_gather(both, axis, axis=0, tiled=True), 0, [])
    for t, dim in zip(turned, dims):
        section = whole[:, at : at + t[0].size].reshape(-1, *t.shape[1:])
        gathered.append(jnp.moveaxis(section, 0, dim))
        at += t[0].size
    return tuple(gathered)


def per_device(
    grad_query,
    grad_key,
    grad_value,
    grad_mixed,
    grad_norm,
    grad_bias,
    weight_query,
    weight_key,
    weight_value,
    weight_mixed,
    weight_norm,
    weight_bias,
):
    mean_query, mean_key, mean_value, mean_mixed, mean_norm, mean_bias = sum_packed(
        (grad_query[0], grad_key[0], grad_value[0], grad_mixed[0], grad_norm[0], grad_bias[0]),
        "batch",
        (0, 0, 0, 1, 0, 0),
    )
    mean_rate = lax.axis_size("batch") ** (-0.5)
    mean_query = mean_query * mean_rate
    mean_key = mean_key * mean_rate
    mean_value = mean_value * mean_rate
    mean_mixed = mean_mixed * mean_rate
    mean_norm = mean_norm * mean_rate
    mean_bias = mean_bias * mean_rate
    (
        own_query,
        own_key,
        own_value,
        own_mixed,
        slope_query_norm,
        slope_key_norm,
        slope_value_norm,
        slope_mixed_norm,
    ) = in_one(
        (
            jnp.sum(weight_query * weight_query, axis=1, keepdims=True),
            jnp.sum(weight_key * weight_key, axis=1, keepdims=True),
            jnp.sum(weight_value * weight_value, axis=1, keepdims=True),
            jnp.sum(weight_mixed * weight_mixed, axis=0, keepdims=True),
            jnp.sum(mean_query * mean_query, axis=1, keepdims=True),
            jnp.sum(mean_key * mean_key, axis=1, keepdims=True),
            jnp.sum(mean_value * mean_value, axis=1, keepdims=True),
            jnp.sum(mean_mixed * mean_mixed, axis=0, keepdims=True),
        ),
        "cols",
    )
    mean_query = mean_query * (jnp.sqrt(own_query) * lax.rsqrt(slope_query_norm + 1e-06))
    mean_key = mean_key * (jnp.sqrt(own_key) * lax.rsqrt(slope_key_norm + 1e-06))
    mean_value = mean_value * (jnp.sqrt(own_value) * lax.rsqrt(slope_value_norm + 1e-06))
    mean_mixed = mean_mixed * (jnp.sqrt(own_mixed) * lax.rsqrt(slope_mixed_norm + 1e-06))
    new_query = weight_query - learn_rate * mean_query
    new_key = weight_key - learn_rate * mean_key
    new_value = weight_value - learn_rate * mean_value
    new_mixed = weight_mixed - learn_rate * mean_mixed
    new_norm = weight_norm - learn_rate * mean_norm
    new_bias = weight_bias - learn_rate * mean_bias
    copy_query, copy_key, copy_value, copy_mixed, copy_norm, copy_bias = gather_turned(
        (
            new_query.astype(jnp.bfloat16),
            new_key.astype(jnp.bfloat16),
            new_value.astype(jnp.bfloat16),
            new_mixed.astype(jnp.bfloat16),
            new_norm.astype(jnp.bfloat16),
            new_bias.astype(jnp.bfloat16),
        ),
        "batch",
        (0, 0, 0, 1, 0, 0),
    )
    return (
        copy_query,
        copy_key,
        copy_value,
        copy_mixed,
        copy_norm,
        copy_bias,
        new_query,
        new_key,
        new_value,
        new_mixed,
        new_norm,
        new_bias,
    )


def solution(mesh):
    in_specs = (
        P("batch", None, "cols"),
        P("batch", None, "cols"),
        P("batch", None, "cols"),
        P("batch", "cols", None),
        P("batch", None),
        P("batch", None),
        P("batch", "cols"),
        P("batch", "cols"),
        P("batch", "cols"),
        P("cols", "batch"),
        P("batch"),
        P("batch"),
    )
    out_specs = (
        P(None, "cols"),
        P(None, "cols"),
        P(None, "cols"),
        P("cols", None),
        P(),
        P(),
        P("batch", "cols"),
        P("batch", "cols"),
        P("batch", "cols"),
        P("cols", "batch"),
        P("batch"),
        P("batch"),
    )
    return jax.shard_map(
        per_device, mesh=mesh, in_specs=in_specs, out_specs=out_specs, check_vma=False
    )
```

profile of v0, /device:TPU:32, one launch (start us, length us, event | category | flops | bytes accessed | tf_op | source)
XLA Modules:
  0.0 223.8 jit_solution(5893439755638786750)
XLA Ops:
  7.2 0.0 all-reduce.4.cloned.1.call-start
  7.2 1.6 reshape_reshape_squeeze.9
  8.8 1.1 constant_dynamic-update-slice_fusion.4
  9.9 0.2 reshape_reshape_squeeze.10
  10.1 0.2 reshape_reshape_squeeze.11
  10.3 0.0 copy-start.7
  10.3 1.4 copy.90
  11.7 1.1 constant_dynamic-update-slice_fusion.3
  12.8 1.1 constant_dynamic-update-slice_fusion.2
  13.8 1.1 bitcast_dynamic-update-slice_fusion
  14.9 0.6 constant_dynamic-update-slice_fusion.1
  15.5 0.6 constant_dynamic-update-slice_fusion
  16.1 4.4 %pad.4 = f32[16,66560]{1,0:T(8,128)} pad(f32[16,65792]{1,0:T(8,128)} %constant_dynamic-update-slice_fusion, f32[]{:T(128)} %constant.5.clone.1), padding=0_0x0_768 | pad | bytes 8470532 | tf_op jit(solution)/shard_map/jit(_pad)/pad | solution.py:20
  20.6 3.9 %reshape.94 = f32[8320,128]{1,0:T(8,128)} reshape(f32[16,66560]{1,0:T(8,128)} %pad.4) | data formatting | bytes 8519680 | tf_op jit(solution)/shard_map/reshape | solution.py:20
  24.5 0.0 all-reduce.4.cloned.1.call-update
  24.6 0.6 copy-done.10
  25.2 0.6 dynamic-slice
  26.4 0.1 copy.68
  26.5 0.1 copy.69
  26.6 0.1 copy.67
  26.7 0.1 multiply_reduce_fusion.7
  26.8 0.1 multiply_reduce_fusion.6
  27.0 0.1 multiply_reduce_fusion.5
  27.1 114.2 %all-reduce.4.cloned.1.call-done = f32[8320,128]{1,0:T(8,128)} async-done(((f32[8320,128]{1,0:T(8,128)}), f32[8320,128]{1,0:T(8,128)}) %all-reduce.4.cloned.1.call-update) | async-done | bytes 4259856
  141.4 1.0 constant_dynamic-slice_fusion.1
  142.4 0.1 copy.78
  142.5 0.1 copy.79
  142.6 0.1 copy.80
  142.8 0.1 copy.65
  142.9 0.1 multiply_reduce_fusion
  143.0 0.7 broadcast_in_dim.3
  143.7 7.5 %all-to-all-start = ((f32[16,1,1024]{2,1,0:T(1,128)}), f32[16,1,1024]{2,1,0:T(1,128)S(1)}, u32[]{:S(2)}, u32[]{:S(2)}) async-start(f32[16,1,1024]{2,1,0:T(1,128)} %broadcast_in_dim.3), calls=%async_computation | async-start | bytes 131072 | tf_op jit(solution)/shard_map/all_to_all | solution.py:31
  151.2 0.0 all-gather.2.cloned.1.call-start
  151.3 1.3 convert_bitcast_fusion.1
  152.5 5.2 %all-to-all-done = f32[16,1,1024]{2,1,0:T(1,128)S(1)} async-done(((f32[16,1,1024]{2,1,0:T(1,128)}), f32[16,1,1024]{2,1,0:T(1,128)S(1)}, u32[]{:S(2)}, u32[]{:S(2)}) %all-to-all-start) | async-done | bytes 65568 | tf_op jit(solution)/shard_map/all_to_all | solution.py:31
  157.7 0.1 reduce_sum.89
  157.8 0.6 convert_bitcast_fusion
  158.5 3.1 %concatenate.11 = bf16[128,514]{0,1:T(8,128)(2,1)} concatenate(bf16[128,128]{0,1:T(8,128)(2,1)S(1)} %get-tuple-element.72, bf16[128,128]{0,1:T(8,128)(2,1)S(1)} %get-tuple-element.88, bf16[128,128]{0,1:T(8,128)(2,1)S(1)} %get-tuple-element.68, bf16[128,128]{0,1:T(8,128)(2,1)S(1)} %get-tuple-element.66, bf16[128,1]{0,1:T(2,128)(2,1)S(1)} %get-tuple-element.74, ...), dimensions={1} | concatenate | bytes 263168 | tf_op jit(solution)/shard_map/concatenate | solution.py:48
  161.6 0.0 all-gather.2.cloned.1.call-update
  161.6 0.7 copy.75
  162.3 0.7 copy.76
  163.0 0.7 copy.74
  163.8 46.3 %all-gather.2.cloned.1.call-done = bf16[2048,514]{0,1:T(8,128)(2,1)} async-done(((bf16[128,514]{0,1:T(8,128)(2,1)}), bf16[2048,514]{0,1:T(8,128)(2,1)}) %all-gather.2.cloned.1.call-update) | async-done | bytes 2105360 | tf_op jit(solution)/shard_map/all_gather | solution.py:49
  210.0 2.5 %slice_bitcast_fusion = (bf16[128,2048]{1,0:T(8,128)(2,1)}, bf16[2048,128]{0,1:T(8,128)(2,1)S(1)}, bf16[2048,128]{0,1:T(8,128)(2,1)S(1)}, bf16[2048,128]{0,1:T(8,128)(2,1)S(1)}) fusion(bf16[2048,514]{0,1:T(8,128)(2,1)} %all-gather.2.cloned.1.call-done), kind=kLoop, calls=%fused_computation.1 | loop fusion | bytes 4194304 | tf_op jit(solution)/shard_map/transpose | solution.py:52
  212.5 1.0 copy.71
  213.5 1.0 copy.72
  214.5 1.0 copy.73
  215.5 1.5 slice_reduce_fusion
  (36 shorter events, 0.3 us)
Async XLA Ops:
  7.2 2.7 %copy-start = (f32[1,2048,128]{2,1,0:T(8,128)S(1)}, f32[1,2048,128]{2,1,0:T(8,128)}, u32[]{:S(2)}) copy-start(f32[1,2048,128]{2,1,0:T(8,128)} %param.13) | copy-start | bytes 3145732
  7.2 2.9 %copy-start.1 = (f32[1,2048,128]{2,1,0:T(8,128)S(1)}, f32[1,2048,128]{2,1,0:T(8,128)}, u32[]{:S(2)}) copy-start(f32[1,2048,128]{2,1,0:T(8,128)} %param.14) | copy-start | bytes 3145732
  7.2 134.2 %all-reduce.4.cloned.1.call-start = ((), (), s32[]{:S(2)}) async-start(), calls=%async_computation.2 | async-start | bytes 8519680
  10.3 4.6 %copy-start.6 = (f32[1,2048]{1,0:T(1,128)S(1)}, f32[1,2048]{1,0:T(1,128)}, u32[]{:S(2)}) copy-start(f32[1,2048]{1,0:T(1,128)} %param.16) | copy-start | bytes 24580
  10.3 5.2 %copy-start.7 = (f32[1,2048]{1,0:T(1,128)S(1)}, f32[1,2048]{1,0:T(1,128)}, u32[]{:S(2)}) copy-start(f32[1,2048]{1,0:T(1,128)} %param.17) | copy-start | bytes 24580
  24.5 0.7 copy-start.10
  24.5 1.9 copy-start.4
  24.5 2.0 copy-start.5
  24.5 2.1 copy-start.3
  24.5 2.6 %copy-start.2 = (f32[128,128]{1,0:T(8,128)S(1)}, f32[128,128]{1,0:T(8,128)}, u32[]{:S(2)}) copy-start(f32[128,128]{1,0:T(8,128)} %param.21) | copy-start | bytes 196612
  24.5 126.7 %copy-start.8 = (f32[128]{0:T(128)S(1)}, f32[128]{0:T(128)}, u32[]{:S(2)}) copy-start(f32[128]{0:T(128)} %param.23) | copy-start | bytes 1540
  24.5 126.7 %copy-start.9 = (f32[128]{0:T(128)S(1)}, f32[128]{0:T(128)}, u32[]{:S(2)}) copy-start(f32[128]{0:T(128)} %param.22) | copy-start | bytes 1540
  143.7 14.0 %all-to-all-start = ((f32[16,1,1024]{2,1,0:T(1,128)}), f32[16,1,1024]{2,1,0:T(1,128)S(1)}, u32[]{:S(2)}, u32[]{:S(2)}) async-start(f32[16,1,1024]{2,1,0:T(1,128)} %broadcast_in_dim.3), calls=%async_computation | async-start | bytes 131072 | tf_op jit(solution)/shard_map/all_to_all | solution.py:31
  151.2 58.8 %all-gather.2.cloned.1.call-start = ((), (), s32[]{:S(2)}) async-start(), calls=%async_computation.1 | async-start | bytes 2263040 | tf_op jit(solution)/shard_map/all_gather | solution.py:49
Sparse Core Ops, SparseCore 0:
  24.7 116.6 all-reduce.3
  161.7 48.2 all-gather.1
where the time goes:
time: 224 us
  waiting for transfers between devices  166 us (74%)
  local copies, waits for them, and re-layouts  32.9 us (15%)
  between operations  15 us (7%)
  starting transfers between devices  7.57 us (3%)
  other arithmetic  2.61 us (1%)
    unnamed x3, waiting for transfers between devices  114 us
    all_gather x1, waiting for transfers between devices, gather_turned(): lax.all_gather(both, axis, axis=0, tiled=True)  46.3 us
    unnamed x48, local copies, waits for them, and re-layouts  13.3 us
    all_to_all x1, starting transfers between devices, from_everyone(): return lax.all_to_all(copies, axis, split_axis=0, concat_axis=0, tiled=True)  7.5 us
    all_to_all x1, waiting for transfers between devices, from_everyone(): return lax.all_to_all(copies, axis, split_axis=0, concat_axis=0, tiled=True)  5.16 us
  transfers between devices with their start and end apart: 3, of which 3 were waited for; matrix products, arithmetic and copies ran while one was open for 2% of the time, Pallas kernels for 0%

commit v1 on v0

v1 whole, which is shorter than its diff:
```python
import jax
import jax.numpy as jnp
from jax import lax
from jax.experimental import pallas as pl
from jax.experimental.pallas import tpu as pltpu
from jax.sharding import PartitionSpec as P

learn_rate = 0.4
mean_rate = 0.25
MESH = pl.DeviceIdType.MESH
SIDE = 4
GROUP = 16
BLOCK = 128
HALF = 64
f32 = jnp.float32
bf16 = jnp.bfloat16

FIRST = ("x", "y", "x", "y")


def row_sums(a):
    return jnp.sum(a.T, axis=0, keepdims=True)


def column_sums(a):
    return jnp.sum(a, axis=0, keepdims=True)


def along_rows(line):
    return jnp.broadcast_to(line, (BLOCK, BLOCK)).T


def along_columns(line):
    return jnp.broadcast_to(line, (BLOCK, BLOCK))


SUMS = (row_sums, row_sums, row_sums, column_sums)
SPREAD = (along_rows, along_rows, along_rows, along_columns)


def kernel(
    gq, gk, gv, gm, gn, gb, wq, wk, wv, wm, wn, wb,
    cq, ck, cv, cm, cnb, nq, nk, nv, nm, nn, nb,
    grad, first_in, total, second_in, whole, weight, fresh,
    own_norms, slope_norms, small_grad, small_in, small_weight, small_new, small_all,
    load_sem, send_sem, recv_sem, norm_send, norm_recv, small_send, small_recv, small_load, out_sem,
):
    b = lax.axis_index("batch")
    c = lax.axis_index("cols")
    y, x = b // SIDE, lax.rem(b, SIDE)
    place = {"y": y, "x": x}

    def neighbour(axis, step):
        p = lax.rem(place[axis] + step + SIDE, SIDE)
        return ((p * SIDE + x) if axis == "y" else (y * SIDE + p), c)

    def at(axis, step):
        return lax.rem(place[axis] + step + SIDE, SIDE)

    loads = {}

    def quarter(t, j):
        return grad.at[t, :, j] if FIRST[t] == "x" else grad.at[t, j]

    def start_load(t, n, j):
        g = (gq, gk, gv, gm)[t]
        if t < 3:
            src = g.at[:, j] if FIRST[t] == "x" else g.at[j]
            copy = pltpu.make_async_copy(src, quarter(t, j), load_sem.at[t, n])
            copy.start()
        else:
            for i in range(SIDE):
                at_column = pl.multiple_of((j * SIDE + i) * BLOCK, BLOCK)
                pltpu.make_async_copy(
                    g.at[:, pl.ds(at_column, BLOCK)], grad.at[t, j, i], load_sem.at[t, n]
                ).start()
            copy = pltpu.make_async_copy(quarter(t, j), quarter(t, j), load_sem.at[t, n])
        loads[t, n] = copy

    steps = (2, 1, -1, 0)
    for pair in (0, 1):
        for n, step in enumerate(steps):
            for t in (2 * pair, 2 * pair + 1):
                start_load(t, n, at(FIRST[t], step))
        if pair == 0:
            weight_copies = []
            for t, w in enumerate((wq, wk, wv, wm)):
                copy = pltpu.make_async_copy(w, weight.at[t], load_sem.at[t, 4])
                copy.start()
                weight_copies.append(copy)
            small_copies = [
                pltpu.make_async_copy(gn, small_grad.at[0], small_load.at[0]),
                pltpu.make_async_copy(gb, small_grad.at[1], small_load.at[1]),
                pltpu.make_async_copy(wn, small_weight.at[pl.ds(0, 1)], small_load.at[2]),
                pltpu.make_async_copy(wb, small_weight.at[pl.ds(1, 1)], small_load.at[3]),
            ]
            for copy in small_copies:
                copy.start()

    barrier = pltpu.get_barrier_semaphore()

    def greet(k, carry):
        other_b = lax.rem(b + k, GROUP)
        other_c = lax.rem(c + k, GROUP)
        pl.semaphore_signal(barrier, inc=1, device_id=(other_b, c), device_id_type=MESH)
        pl.semaphore_signal(barrier, inc=1, device_id=(b, other_c), device_id_type=MESH)
        return carry

    lax.fori_loop(1, GROUP, greet, 0)
    pl.semaphore_wait(barrier, 2 * (GROUP - 1))

    sent = []

    def send(t, n, src, dst, device):
        copy = pltpu.make_async_remote_copy(
            src_ref=src,
            dst_ref=dst,
            send_sem=send_sem.at[t, n],
            recv_sem=recv_sem.at[t, n],
            device_id=device,
            device_id_type=MESH,
        )
        copy.start()
        sent.append(copy)
        return copy

    def q1(t, j, h):
        return grad.at[t, pl.ds(2 * h, 2), j] if FIRST[t] == "x" else grad.at[t, j, pl.ds(2 * h, 2)]

    def v1(t, j, h):
        return grad[t, pl.ds(2 * h, 2), j] if FIRST[t] == "x" else grad[t, j, pl.ds(2 * h, 2)]

    def other(t):
        return "y" if FIRST[t] == "x" else "x"

    flight = {}

    def stage1_open(t):
        a = FIRST[t]
        up, down = neighbour(a, 1), neighbour(a, -1)
        loads[t, 0].wait()
        flight[t, 0] = send(t, 0, q1(t, at(a, 2), 0), first_in.at[t, 0], up)
        flight[t, 1] = send(t, 1, q1(t, at(a, 2), 1), first_in.at[t, 1], down)
        loads[t, 1].wait()
        flight[t, 2] = send(t, 2, q1(t, at(a, 1), 1), first_in.at[t, 2], up)
        loads[t, 2].wait()
        flight[t, 3] = send(t, 3, q1(t, at(a, -1), 0), first_in.at[t, 3], down)

    def stage1_relay(t):
        a = FIRST[t]
        up, down = neighbour(a, 1), neighbour(a, -1)
        flight[t, 0].wait_recv()
        first_in[t, 0] = first_in[t, 0] + v1(t, at(a, 1), 0)
        flight[t, 4] = send(t, 4, first_in.at[t, 0], first_in.at[t, 4], up)
        flight[t, 1].wait_recv()
        first_in[t, 1] = first_in[t, 1] + v1(t, at(a, -1), 1)
        flight[t, 5] = send(t, 5, first_in.at[t, 1], first_in.at[t, 5], down)

    def stage1_close(t):
        a = FIRST[t]
        for n in (2, 3, 4, 5):
            flight[t, n].wait_recv()
        loads[t, 3].wait()
        total[t, pl.ds(0, 2)] = v1(t, at(a, 0), 0) + first_in[t, 3] + first_in[t, 4]
        total[t, pl.ds(2, 2)] = v1(t, at(a, 0), 1) + first_in[t, 2] + first_in[t, 5]

    def rows(h):
        return pl.ds(HALF * h, HALF)

    def stage2_open(t):
        a = other(t)
        up, down = neighbour(a, 1), neighbour(a, -1)
        flight[t, 6] = send(t, 6, total.at[t, at(a, 2), rows(0)], second_in.at[t, 0], up)
        flight[t, 7] = send(t, 7, total.at[t, at(a, 2), rows(1)], second_in.at[t, 1], down)
        flight[t, 8] = send(t, 8, total.at[t, at(a, 1), rows(1)], second_in.at[t, 2], up)
        flight[t, 9] = send(t, 9, total.at[t, at(a, -1), rows(0)], second_in.at[t, 3], down)

    def stage2_relay(t):
        a = other(t)
        up, down = neighbour(a, 1), neighbour(a, -1)
        flight[t, 6].wait_recv()
        second_in[t, 0] = second_in[t, 0] + total[t, at(a, 1), rows(0)]
        flight[t, 10] = send(t, 10, second_in.at[t, 0], second_in.at[t, 4], up)
        flight[t, 7].wait_recv()
        second_in[t, 1] = second_in[t, 1] + total[t, at(a, -1), rows(1)]
        flight[t, 11] = send(t, 11, second_in.at[t, 1], second_in.at[t, 5], down)

    def stage2_close(t):
        a = other(t)
        for n in (8, 9, 10, 11):
            flight[t, n].wait_recv()
        top = total[t, at(a, 0), rows(0)] + second_in[t, 3] + second_in[t, 4]
        bottom = total[t, at(a, 0), rows(1)] + second_in[t, 2] + second_in[t, 5]
        mean = jnp.concatenate([top, bottom], axis=0) * mean_rate
        fresh[t] = mean
        return SUMS[t](mean * mean)

    def to_cols(buffer, n):
        def one(k, carry):
            peer = lax.rem(c + k, GROUP)
            pltpu.make_async_remote_copy(
                src_ref=buffer.at[c],
                dst_ref=buffer.at[c],
                send_sem=norm_send.at[n],
                recv_sem=norm_recv.at[n],
                device_id=(b, peer),
                device_id_type=MESH,
            ).start()
            return carry

        lax.fori_loop(1, GROUP, one, 0)

    def wait_fifteen(buffer, sem):
        part = buffer.at[pl.ds(0, GROUP - 1)]
        pltpu.make_async_copy(part, part, sem).wait()

    def line(t, j):
        return whole.at[t, :, j] if FIRST[t] == "x" else whole.at[t, j]

    def block(t, axis, j):
        return whole.at[t, j, x] if axis == "y" else whole.at[t, y, j]

    def gather_open(t):
        a = other(t)
        own = whole.at[t, y, x]
        flight[t, 12] = send(t, 12, own, own, neighbour(a, 1))
        flight[t, 13] = send(t, 13, own, own, neighbour(a, -1))

    def gather_relay(t):
        a = other(t)
        flight[t, 12].wait_recv()
        src = block(t, a, at(a, -1)).at[rows(0)]
        flight[t, 14] = send(t, 14, src, src, neighbour(a, 1))
        flight[t, 13].wait_recv()
        src = block(t, a, at(a, 1)).at[rows(1)]
        flight[t, 15] = send(t, 15, src, src, neighbour(a, -1))

    def gather_line(t):
        a = FIRST[t]
        flight[t, 14].wait_recv()
        flight[t, 15].wait_recv()
        own = line(t, at(a, 0))
        flight[t, 16] = send(t, 16, own, own, neighbour(a, 1))
        flight[t, 17] = send(t, 17, own, own, neighbour(a, -1))
        write_out(t, at(a, 0))

    def gather_line_relay(t):
        a = FIRST[t]
        flight[t, 16].wait_recv()
        src = line(t, at(a, -1)).at[pl.ds(0, 2)]
        flight[t, 18] = send(t, 18, src, src, neighbour(a, 1))
        flight[t, 17].wait_recv()
        src = line(t, at(a, 1)).at[pl.ds(2, 2)]
        flight[t, 19] = send(t, 19, src, src, neighbour(a, -1))
        write_out(t, at(a, -1))
        write_out(t, at(a, 1))

    def gather_close(t):
        flight[t, 18].wait_recv()
        flight[t, 19].wait_recv()
        write_out(t, at(FIRST[t], 2))

    def write_out(t, j):
        out = (cq, ck, cv, cm)[t]
        if t < 3:
            dst = out.at[:, j] if FIRST[t] == "x" else out.at[j]
            pltpu.make_async_copy(line(t, j), dst, out_sem.at[t]).start()
        else:
            for i in range(SIDE):
                at_column = pl.multiple_of((j * SIDE + i) * BLOCK, BLOCK)
                pltpu.make_async_copy(
                    whole.at[t, j, i], out.at[:, pl.ds(at_column, BLOCK)], out_sem.at[t]
                ).start()

    stage1_open(0)
    stage1_open(1)

    for copy in small_copies:
        copy.wait()

    def small_out(k, carry):
        peer = lax.rem(b + k, GROUP)
        at_lane = pl.multiple_of(peer * BLOCK, BLOCK)
        for i in (0, 1):
            pltpu.make_async_remote_copy(
                src_ref=small_grad.at[i, :, pl.ds(at_lane, BLOCK)],
                dst_ref=small_in.at[b, pl.ds(i, 1)],
                send_sem=small_send.at[0],
                recv_sem=small_recv.at[0],
                device_id=(peer, c),
                device_id_type=MESH,
            ).start()
        return carry

    lax.fori_loop(1, GROUP, small_out, 0)
    own_lane = pl.multiple_of(b * BLOCK, BLOCK)
    small_in[b, pl.ds(0, 1)] = small_grad[0, :, pl.ds(own_lane, BLOCK)]
    small_in[b, pl.ds(1, 1)] = small_grad[1, :, pl.ds(own_lane, BLOCK)]

    for t in range(4):
        weight_copies[t].wait()
        own_norms[c, pl.ds(t, 1)] = SUMS[t](weight[t] * weight[t])
    to_cols(own_norms, 0)

    stage1_relay(0)
    stage1_relay(1)
    stage1_open(2)
    stage1_open(3)

    wait_fifteen(small_in, small_recv.at[0])
    small_sum = small_in[0]
    for i in range(1, GROUP):
        small_sum = small_sum + small_in[i]
    small_step = small_weight[...] - learn_rate * (small_sum * mean_rate)
    small_new[...] = small_step
    small_all[b] = small_step

    def small_back(k, carry):
        pltpu.make_async_remote_copy(
            src_ref=small_new,
            dst_ref=small_all.at[b],
            send_sem=small_send.at[1],
            recv_sem=small_recv.at[1],
            device_id=(lax.rem(b + k, GROUP), c),
            device_id_type=MESH,
        ).start()
        return carry

    lax.fori_loop(1, GROUP, small_back, 0)

    def norms_out(pair):
        for i in (0, 1):
            slope_norms[pair, c, pl.ds(i, 1)] = stage2_close(2 * pair + i)
        to_cols(slope_norms.at[pair], 1 + pair)

    def step(pair):
        wait_fifteen(slope_norms.at[pair], norm_recv.at[1 + pair])
        slopes = jnp.sum(slope_norms[pair], axis=0)
        for i in (0, 1):
            t = 2 * pair + i
            ratio = jnp.sqrt(own_sum[t : t + 1]) * lax.rsqrt(slopes[i : i + 1] + 1e-06)
            new = weight[t] - learn_rate * (fresh[t] * SPREAD[t](ratio))
            fresh[t] = new
            whole[t, y, x] = new.astype(bf16)
        for i in (0, 1):
            t = 2 * pair + i
            gather_open(t)
            copy = pltpu.make_async_copy(fresh.at[t], (nq, nk, nv, nm)[t], out_sem.at[4 + t])
            copy.start()
            new_copies.append(copy)

    new_copies = []
    stage1_close(0)
    stage2_open(0)
    stage1_close(1)
    stage2_open(1)

    stage1_relay(2)
    stage1_relay(3)
    stage2_relay(0)
    stage2_relay(1)
    norms_out(0)

    wait_fifteen(own_norms, norm_recv.at[0])
    own_sum = jnp.sum(own_norms[...], axis=0)

    stage1_close(2)
    stage2_open(2)
    stage1_close(3)
    stage2_open(3)
    step(0)
    stage2_relay(2)
    stage2_relay(3)
    gather_relay(0)
    gather_relay(1)
    norms_out(1)
    gather_line(0)
    gather_line(1)
    step(1)
    gather_relay(2)
    gather_relay(3)
    gather_line_relay(0)
    gather_line_relay(1)
    gather_line(2)
    gather_line(3)
    gather_close(0)
    gather_close(1)

    wait_fifteen(small_all, small_recv.at[1])
    tail = [
        pltpu.make_async_copy(small_all, cnb, small_load.at[0]),
        pltpu.make_async_copy(small_new.at[pl.ds(0, 1)], nn, small_load.at[1]),
        pltpu.make_async_copy(small_new.at[pl.ds(1, 1)], nb, small_load.at[2]),
    ]
    for copy in tail:
        copy.start()

    gather_line_relay(2)
    gather_line_relay(3)
    gather_close(2)
    gather_close(3)

    for copy in sent:
        copy.wait_send()
    for n, buffer in ((0, own_norms), (1, slope_norms.at[0]), (2, slope_norms.at[1])):
        wait_fifteen(buffer, norm_send.at[n])
    wait_fifteen(small_in, small_send.at[0])
    wait_fifteen(small_all, small_send.at[1])
    for t in range(4):
        pltpu.make_async_copy(whole.at[t], whole.at[t], out_sem.at[t]).wait()
    for copy in new_copies + tail:
        copy.wait()


def per_device(gq, gk, gv, gm, gn, gb, wq, wk, wv, wm, wn, wb):
    blocks = (SIDE, SIDE, BLOCK, BLOCK)
    any_space = pl.BlockSpec(memory_space=pl.ANY)
    shape = jax.ShapeDtypeStruct
    outs = pl.pallas_call(
        kernel,
        out_shape=(
            shape(blocks, bf16),
            shape(blocks, bf16),
            shape(blocks, bf16),
            shape((BLOCK, GROUP * BLOCK), bf16),
            shape((GROUP, 2, BLOCK), f32),
            shape((BLOCK, BLOCK), f32),
            shape((BLOCK, BLOCK), f32),
            shape((BLOCK, BLOCK), f32),
            shape((BLOCK, BLOCK), f32),
            shape((1, BLOCK), f32),
            shape((1, BLOCK), f32),
        ),
        in_specs=[any_space] * 12,
        out_specs=(any_space,) * 11,
        scratch_shapes=[
            pltpu.VMEM((4, SIDE, SIDE, BLOCK, BLOCK), f32),
            pltpu.VMEM((4, 6, 2, BLOCK, BLOCK), f32),
            pltpu.VMEM((4, SIDE, BLOCK, BLOCK), f32),
            pltpu.VMEM((4, 6, HALF, BLOCK), f32),
            pltpu.VMEM((4, SIDE, SIDE, BLOCK, BLOCK), bf16),
            pltpu.VMEM((4, BLOCK, BLOCK), f32),
            pltpu.VMEM((4, BLOCK, BLOCK), f32),
            pltpu.VMEM((GROUP, 4, BLOCK), f32),
            pltpu.VMEM((2, GROUP, 2, BLOCK), f32),
            pltpu.VMEM((2, 1, GROUP * BLOCK), f32),
            pltpu.VMEM((GROUP, 2, BLOCK), f32),
            pltpu.VMEM((2, BLOCK), f32),
            pltpu.VMEM((2, BLOCK), f32),
            pltpu.VMEM((GROUP, 2, BLOCK), f32),
            pltpu.SemaphoreType.DMA((4, 5)),
            pltpu.SemaphoreType.DMA((4, 20)),
            pltpu.SemaphoreType.DMA((4, 20)),
            pltpu.SemaphoreType.DMA((3,)),
            pltpu.SemaphoreType.DMA((3,)),
            pltpu.SemaphoreType.DMA((2,)),
            pltpu.SemaphoreType.DMA((2,)),
            pltpu.SemaphoreType.DMA((4,)),
            pltpu.SemaphoreType.DMA((8,)),
        ],
        compiler_params=pltpu.CompilerParams(collective_id=0, has_side_effects=True),
        name="step",
    )(
        gq.reshape(blocks), gk.reshape(blocks), gv.reshape(blocks), gm[0], gn, gb,
        wq, wk, wv, wm, wn.reshape(1, BLOCK), wb.reshape(1, BLOCK),
    )
    cq, ck, cv, cm, cnb, nq, nk, nv, nm, nn, nb = outs
    whole = (GROUP * BLOCK, BLOCK)
    small = cnb.astype(bf16)
    return (
        cq.reshape(whole), ck.reshape(whole), cv.reshape(whole), cm,
        small[:, 0].reshape(-1), small[:, 1].reshape(-1),
        nq, nk, nv, nm, nn.reshape(-1), nb.reshape(-1),
    )


def solution(mesh):
    cut = P("batch", "cols")
    in_specs = (
        P("batch", None, "cols"), P("batch", None, "cols"), P("batch", None, "cols"), P("batch", "cols", None),
        P("batch", None), P("batch", None), cut, cut, cut, P("cols", "batch"), P("batch"), P("batch"),
    )
    out_specs = (
        P(None, "cols"), P(None, "cols"), P(None, "cols"), P("cols", None), P(), P(),
        cut, cut, cut, P("cols", "batch"), P("batch"), P("batch"),
    )
    return jax.shard_map(per_device, mesh=mesh, in_specs=in_specs, out_specs=out_specs, check_vma=False)
```

time: 224 us -> 75.7 us (0.34)
  waiting for transfers between devices: 166 us -> 0 us
  Pallas kernels: 0 us -> 63.5 us
  local copies, waits for them, and re-layouts: 32.9 us -> 10.3 us
  between operations: 15 us -> 0.67 us
  starting transfers between devices: 7.57 us -> 0 us
    unnamed x3 -> x0, waiting for transfers between devices: 114 us -> none
    pallas_call x0 -> x1, Pallas kernels: none -> 63.5 us  [per_device(): pl.pallas_call(kernel, out_shape=(shape(blocks, bf16), shape(blocks, bf16...]
    all_gather x1 -> x0, waiting for transfers between devices: 46.3 us -> none  [gather_turned(): lax.all_gather(both, axis, axis=0, tiled=True)]
    all_to_all x1 -> x0, starting transfers between devices: 7.5 us -> none  [from_everyone(): return lax.all_to_all(copies, axis, split_axis=0, concat_axis=0, tiled=True)]
    all_to_all x1 -> x0, waiting for transfers between devices: 5.16 us -> none  [from_everyone(): return lax.all_to_all(copies, axis, split_axis=0, concat_axis=0, tiled=True)]
    pad x1 -> x0, local copies, waits for them, and re-layouts: 4.43 us -> none  [sum_packed(): jnp.pad(lines, ((0, 0), (0, rows * 128 - lines.shape[1]))).reshape(-1, 128)]
    reshape x1 -> x0, local copies, waits for them, and re-layouts: 3.93 us -> none  [sum_packed(): jnp.pad(lines, ((0, 0), (0, rows * 128 - lines.shape[1]))).reshape(-1, 128)]
    concatenate x3 -> x0, local copies, waits for them, and re-layouts: 3.7 us -> none  [the longest x1 3.09 us: gather_turned(): both = jnp.concatenate([t.reshape(len(t), -1) for t in turned], axis=1)]
  transfers between devices with their start and end apart: 3 -> 0, of which waited for: 3 -> 0; matrix products, arithmetic and copies ran while one was open for 2% -> 0% of each run, Pallas kernels for 0% -> 0%
where the time goes in v1:
time: 75.7 us; the launch traced here: 75.2 us
  Pallas kernels  63.5 us (84%)
  local copies, waits for them, and re-layouts  10.3 us (14%)
    pallas_call x1, Pallas kernels, per_device(): pl.pallas_call(kernel, out_shape=(shape(blocks, bf16), shape(blocks, bf16...  63.5 us
    unnamed x28, local copies, waits for them, and re-layouts  9.63 us

profile of v1, /device:TPU:32, one launch (start us, length us, event | category | flops | bytes accessed | tf_op | source)
XLA Modules:
  0.0 75.2 jit_solution(15638295659454993531)
XLA Ops:
  0.6 63.5 %step.1 = (bf16[4,4,128,128]{3,2,1,0:T(8,128)(2,1)}, bf16[4,4,128,128]{3,2,1,0:T(8,128)(2,1)}, bf16[4,4,128,128]{3,2,1,0:T(8,128)(2,1)}, bf16[128,2048]{1,0:T(8,...) custom-call(f32[4,4,128,128]{3,2,1,0:T(8,128)} %bitcast.13, ...), custom_call_target="tpu_custom_call" | custom-call | tf_op jit(solution)/shard_map/step/pallas_call | solution.py:419
  64.2 0.7 convert_element_type.3
  64.9 0.6 slice_reduce_fusion
  65.6 0.0 copy-start.2
  65.6 1.9 %copy.34 = bf16[2048,128]{1,0:T(8,128)(2,1)} copy(bf16[2048,128]{1,0:T(8,128)(2,1)} %bitcast.19) | data formatting | bytes 1048576
  67.5 0.0 copy-done.2
  67.5 0.0 copy-start.1
  67.5 0.8 %copy.35 = bf16[2048,128]{1,0:T(8,128)(2,1)} copy(bf16[2048,128]{1,0:T(8,128)(2,1)S(1)} %bitcast.18) | data formatting | bytes 1048576
  68.3 0.4 copy-done.1
  68.7 0.0 copy-start
  68.7 0.8 %copy.36 = bf16[2048,128]{1,0:T(8,128)(2,1)} copy(bf16[2048,128]{1,0:T(8,128)(2,1)S(1)} %bitcast.17) | data formatting | bytes 1048576
  69.5 0.4 copy-done
  70.0 0.0 copy-start.6
  70.0 0.8 %copy.37 = bf16[128,2048]{1,0:T(8,128)(2,1)} copy(bf16[128,2048]{1,0:T(8,128)(2,1)S(1)} %copy-done) | data formatting | bytes 1048576
  70.7 0.1 copy-done.6
  70.8 0.0 copy-start.5
  70.8 0.6 copy.38
  71.4 0.2 copy-done.5
  71.7 0.0 copy-start.4
  71.7 0.6 copy.39
  72.3 0.2 copy-done.4
  72.5 0.0 copy-start.3
  72.5 0.6 copy.40
  73.2 0.2 copy-done.3
  73.4 0.0 copy-start.8
  73.4 0.6 copy.41
  74.0 0.0 copy-done.8
  74.0 0.0 copy-start.7
  74.0 0.5 copy.42
  74.6 0.1 copy-done.7
  74.7 0.5 copy.43
Async XLA Ops:
  65.6 1.9 %copy-start.2 = (bf16[4,4,128,128]{3,2,1,0:T(8,128)(2,1)S(1)}, bf16[4,4,128,128]{3,2,1,0:T(8,128)(2,1)}, u32[]{:S(2)}) copy-start(bf16[4,4,128,128]{3,2,1,0:T(8,128)(2,1)} %get-tuple-element.24) | copy-start | bytes 1572868
  67.5 1.2 %copy-start.1 = (bf16[4,4,128,128]{3,2,1,0:T(8,128)(2,1)S(1)}, bf16[4,4,128,128]{3,2,1,0:T(8,128)(2,1)}, u32[]{:S(2)}) copy-start(bf16[4,4,128,128]{3,2,1,0:T(8,128)(2,1)} %get-tuple-element.25) | copy-start | bytes 1572868
  68.7 1.2 %copy-start = (bf16[128,2048]{1,0:T(8,128)(2,1)S(1)}, bf16[128,2048]{1,0:T(8,128)(2,1)}, u32[]{:S(2)}) copy-start(bf16[128,2048]{1,0:T(8,128)(2,1)} %get-tuple-element.51) | copy-start | bytes 1572868
  70.0 0.9 %copy-start.6 = (f32[128,128]{1,0:T(8,128)S(1)}, f32[128,128]{1,0:T(8,128)}, u32[]{:S(2)}) copy-start(f32[128,128]{1,0:T(8,128)} %get-tuple-element.54) | copy-start | bytes 196612
  70.8 0.9 %copy-start.5 = (f32[128,128]{1,0:T(8,128)S(1)}, f32[128,128]{1,0:T(8,128)}, u32[]{:S(2)}) copy-start(f32[128,128]{1,0:T(8,128)} %get-tuple-element.55) | copy-start | bytes 196612
  71.7 0.9 %copy-start.4 = (f32[128,128]{1,0:T(8,128)S(1)}, f32[128,128]{1,0:T(8,128)}, u32[]{:S(2)}) copy-start(f32[128,128]{1,0:T(8,128)} %get-tuple-element.56) | copy-start | bytes 196612
  72.5 0.9 %copy-start.3 = (f32[128,128]{1,0:T(8,128)S(1)}, f32[128,128]{1,0:T(8,128)}, u32[]{:S(2)}) copy-start(f32[128,128]{1,0:T(8,128)} %get-tuple-element.57) | copy-start | bytes 196612
  73.4 0.6 copy-start.8
  74.0 0.7 copy-start.7

commit v2 on v1

--- a/solution.py
+++ b/solution.py
@@ -40,10 +40,10 @@
 
 def kernel(
     gq, gk, gv, gm, gn, gb, wq, wk, wv, wm, wn, wb,
-    cq, ck, cv, cm, cnb, nq, nk, nv, nm, nn, nb,
-    grad, first_in, total, second_in, whole, weight, fresh,
-    own_norms, slope_norms, small_grad, small_in, small_weight, small_new, small_all,
-    load_sem, send_sem, recv_sem, norm_send, norm_recv, small_send, small_recv, small_load, out_sem,
+    whole, fresh, small_all, small_new,
+    grad, first_in, total, second_in, weight,
+    own_norms, slope_norms, small_grad, small_in, small_weight,
+    load_sem, send_sem, recv_sem, norm_send, norm_recv, small_send, small_recv, small_load,
 ):
     b = lax.axis_index("batch")
     c = lax.axis_index("cols")
@@ -242,7 +242,6 @@
         own = line(t, at(a, 0))
         flight[t, 16] = send(t, 16, own, own, neighbour(a, 1))
         flight[t, 17] = send(t, 17, own, own, neighbour(a, -1))
-        write_out(t, at(a, 0))
 
     def gather_line_relay(t):
         a = FIRST[t]
@@ -252,25 +251,10 @@
         flight[t, 17].wait_recv()
         src = line(t, at(a, 1)).at[pl.ds(2, 2)]
         flight[t, 19] = send(t, 19, src, src, neighbour(a, -1))
-        write_out(t, at(a, -1))
-        write_out(t, at(a, 1))
 
     def gather_close(t):
         flight[t, 18].wait_recv()
         flight[t, 19].wait_recv()
-        write_out(t, at(FIRST[t], 2))
-
-    def write_out(t, j):
-        out = (cq, ck, cv, cm)[t]
-        if t < 3:
-            dst = out.at[:, j] if FIRST[t] == "x" else out.at[j]
-            pltpu.make_async_copy(line(t, j), dst, out_sem.at[t]).start()
-        else:
-            for i in range(SIDE):
-                at_column = pl.multiple_of((j * SIDE + i) * BLOCK, BLOCK)
-                pltpu.make_async_copy(
-                    whole.at[t, j, i], out.at[:, pl.ds(at_column, BLOCK)], out_sem.at[t]
-                ).start()
 
     stage1_open(0)
     stage1_open(1)
@@ -345,11 +329,7 @@
         for i in (0, 1):
             t = 2 * pair + i
             gather_open(t)
-            copy = pltpu.make_async_copy(fresh.at[t], (nq, nk, nv, nm)[t], out_sem.at[4 + t])
-            copy.start()
-            new_copies.append(copy)
-
-    new_copies = []
+
     stage1_close(0)
     stage2_open(0)
     stage1_close(1)
@@ -387,14 +367,6 @@
     gather_close(1)
 
     wait_fifteen(small_all, small_recv.at[1])
-    tail = [
-        pltpu.make_async_copy(small_all, cnb, small_load.at[0]),
-        pltpu.make_async_copy(small_new.at[pl.ds(0, 1)], nn, small_load.at[1]),
-        pltpu.make_async_copy(small_new.at[pl.ds(1, 1)], nb, small_load.at[2]),
-    ]
-    for copy in tail:
-        copy.start()
-
     gather_line_relay(2)
     gather_line_relay(3)
     gather_close(2)
@@ -406,48 +378,56 @@
         wait_fifteen(buffer, norm_send.at[n])
     wait_fifteen(small_in, small_send.at[0])
     wait_fifteen(small_all, small_send.at[1])
-    for t in range(4):
-        pltpu.make_async_copy(whole.at[t], whole.at[t], out_sem.at[t]).wait()
-    for copy in new_copies + tail:
+
+def write_out(whole, fresh, small_all, small_own, cq, ck, cv, cm, cn, cb, nq, nk, nv, nm, nn, nb, small, sem):
+    copies = []
+
+    def start(src, dst):
+        copy = pltpu.make_async_copy(src, dst, sem.at[len(copies)])
+        copy.start()
+        copies.append(copy)
+
+    for t, out in enumerate((cq, ck, cv)):
+        start(whole.at[t], out)
+    for j in range(GROUP):
+        start(whole.at[3, j // SIDE, j % SIDE], cm.at[:, pl.ds(j * BLOCK, BLOCK)])
+    for t, out in enumerate((nq, nk, nv, nm)):
+        start(fresh.at[t], out)
+    for i, out in enumerate((nn, nb)):
+        start(small_own.at[pl.ds(i, 1)], out)
+    for i, out in enumerate((cn, cb)):
+        small[i] = small_all[:, i].astype(bf16)
+        start(small.at[i], out)
+    for copy in copies:
         copy.wait()
 
 
 def per_device(gq, gk, gv, gm, gn, gb, wq, wk, wv, wm, wn, wb):
     blocks = (SIDE, SIDE, BLOCK, BLOCK)
     any_space = pl.BlockSpec(memory_space=pl.ANY)
+    in_place = pl.BlockSpec(memory_space=pltpu.VMEM)
     shape = jax.ShapeDtypeStruct
-    outs = pl.pallas_call(
+    results = pl.pallas_call(
         kernel,
         out_shape=(
-            shape(blocks, bf16),
-            shape(blocks, bf16),
-            shape(blocks, bf16),
-            shape((BLOCK, GROUP * BLOCK), bf16),
-            shape((GROUP, 2, BLOCK), f32),
-            shape((BLOCK, BLOCK), f32),
-            shape((BLOCK, BLOCK), f32),
-            shape((BLOCK, BLOCK), f32),
-            shape((BLOCK, BLOCK), f32),
-            shape((1, BLOCK), f32),
-            shape((1, BLOCK), f32),
+            pltpu.VMEM((4, *blocks), bf16),
+            pltpu.VMEM((4, BLOCK, BLOCK), f32),
+            pltpu.VMEM((GROUP, 2, BLOCK), f32),
+            pltpu.VMEM((2, BLOCK), f32),
         ),
         in_specs=[any_space] * 12,
-        out_specs=(any_space,) * 11,
+        out_specs=(in_place,) * 4,
         scratch_shapes=[
-            pltpu.VMEM((4, SIDE, SIDE, BLOCK, BLOCK), f32),
+            pltpu.VMEM((4, *blocks), f32),
             pltpu.VMEM((4, 6, 2, BLOCK, BLOCK), f32),
             pltpu.VMEM((4, SIDE, BLOCK, BLOCK), f32),
             pltpu.VMEM((4, 6, HALF, BLOCK), f32),
-            pltpu.VMEM((4, SIDE, SIDE, BLOCK, BLOCK), bf16),
-            pltpu.VMEM((4, BLOCK, BLOCK), f32),
             pltpu.VMEM((4, BLOCK, BLOCK), f32),
             pltpu.VMEM((GROUP, 4, BLOCK), f32),
             pltpu.VMEM((2, GROUP, 2, BLOCK), f32),
             pltpu.VMEM((2, 1, GROUP * BLOCK), f32),
             pltpu.VMEM((GROUP, 2, BLOCK), f32),
             pltpu.VMEM((2, BLOCK), f32),
-            pltpu.VMEM((2, BLOCK), f32),
-            pltpu.VMEM((GROUP, 2, BLOCK), f32),
             pltpu.SemaphoreType.DMA((4, 5)),
             pltpu.SemaphoreType.DMA((4, 20)),
             pltpu.SemaphoreType.DMA((4, 20)),
@@ -456,20 +436,36 @@
             pltpu.SemaphoreType.DMA((2,)),
             pltpu.SemaphoreType.DMA((2,)),
             pltpu.SemaphoreType.DMA((4,)),
-            pltpu.SemaphoreType.DMA((8,)),
         ],
-        compiler_params=pltpu.CompilerParams(collective_id=0, has_side_effects=True),
+        compiler_params=pltpu.CompilerParams(
+            collective_id=0, has_side_effects=True, vmem_limit_bytes=24 * 1024 * 1024
+        ),
         name="step",
-    )(
-        gq.reshape(blocks), gk.reshape(blocks), gv.reshape(blocks), gm[0], gn, gb,
-        wq, wk, wv, wm, wn.reshape(1, BLOCK), wb.reshape(1, BLOCK),
-    )
-    cq, ck, cv, cm, cnb, nq, nk, nv, nm, nn, nb = outs
+    )(*(
+        pltpu.with_memory_space_constraint(a, pltpu.HBM)
+        for a in (
+            gq.reshape(blocks), gk.reshape(blocks), gv.reshape(blocks), gm[0], gn, gb,
+            wq, wk, wv, wm, wn.reshape(1, BLOCK), wb.reshape(1, BLOCK),
+        )
+    ))
+    cq, ck, cv, cm, cn, cb, nq, nk, nv, nm, nn, nb = pl.pallas_call(
+        write_out,
+        out_shape=(
+            shape(blocks, bf16), shape(blocks, bf16), shape(blocks, bf16), shape((BLOCK, GROUP * BLOCK), bf16),
+            shape((GROUP, BLOCK), bf16), shape((GROUP, BLOCK), bf16),
+            shape((BLOCK, BLOCK), f32), shape((BLOCK, BLOCK), f32), shape((BLOCK, BLOCK), f32), shape((BLOCK, BLOCK), f32),
+            shape((1, BLOCK), f32), shape((1, BLOCK), f32),
+        ),
+        in_specs=[in_place] * 4,
+        out_specs=(any_space,) * 12,
+        scratch_shapes=[pltpu.VMEM((2, GROUP, BLOCK), bf16), pltpu.SemaphoreType.DMA((32,))],
+        compiler_params=pltpu.CompilerParams(vmem_limit_bytes=8 * 1024 * 1024),
+        name="write_out",
+    )(*(pltpu.with_memory_space_constraint(a, pltpu.VMEM) for a in results))
     whole = (GROUP * BLOCK, BLOCK)
-    small = cnb.astype(bf16)
     return (
         cq.reshape(whole), ck.reshape(whole), cv.reshape(whole), cm,
-        small[:, 0].reshape(-1), small[:, 1].reshape(-1),
+        cn.reshape(-1), cb.reshape(-1),
         nq, nk, nv, nm, nn.reshape(-1), nb.reshape(-1),
     )
 

time: 75.7 us -> 65.3 us (0.86)
  local copies, waits for them, and re-layouts: 10.3 us -> 0 us
  Pallas kernels: 63.5 us -> 64.6 us
    unnamed x28 -> x0, local copies, waits for them, and re-layouts: 9.63 us -> none
    pallas_call x1 -> x2, Pallas kernels: 63.5 us -> 64.6 us  [the longest x1 62.9 us: per_device(): pl.pallas_call(kernel, out_shape=(pltpu.VMEM((4, *blocks), bf16), pltpu.V...]
where the time goes in v2:
time: 65.3 us; the launch traced here: 65.2 us
  Pallas kernels  64.6 us (99%)
  between operations  0.66 us (1%)
    pallas_call x1, Pallas kernels, per_device(): pl.pallas_call(kernel, out_shape=(pltpu.VMEM((4, *blocks), bf16), pltpu.V...  62.9 us
    pallas_call x1, Pallas kernels, per_device(): pl.pallas_call(write_out, out_shape=(shape(blocks, bf16), shape(blocks, b...  1.68 us

profile of v2, /device:TPU:32, one launch (start us, length us, event | category | flops | bytes accessed | tf_op | source)
XLA Modules:
  0.0 65.2 jit_solution(7893383745436603851)
XLA Ops:
  0.6 62.9 %step.1 = (bf16[4,4,4,128,128]{4,3,2,1,0:T(8,128)(2,1)S(1)}, f32[4,128,128]{2,1,0:T(8,128)S(1)}, f32[16,2,128]{2,1,0:T(2,128)S(1)}, f32[2,128]{1,0:T(2,128)S(1)}) custom-call(f32[4,4,128,128]{3,2,1,0:T(8,128)} %bitcast.13, f32[4,4,128,128]{3,2,1,0:T(8,128)} %bitcast.14, f32[4,4,128,128]{3,2,1,0:T(8,128)} %bitcast.15, f32[128,2048]{1,0:T(8,128)} %bitcast.16, ...), custom_call_target="tpu_custom_call" | custom-call | tf_op jit(solution)/shard_map/step/pallas_call | solution.py:410
  63.6 1.7 %write_out.1 = (bf16[4,4,128,128]{3,2,1,0:T(8,128)(2,1)}, bf16[4,4,128,128]{3,2,1,0:T(8,128)(2,1)}, bf16[4,4,128,128]{3,2,1,0:T(8,128)(2,1)}, bf16[128,2048]{1,0...) custom-call(bf16[4,4,4,128,128]{4,3,2,1,0:T(8,128)(2,1)S(1)} %get-tu, ...), custom_call_target="tpu_custom_call" | custom-call | tf_op jit(solution)/shard_map/write_out/pallas_call | solution.py:451

commit v3 on v2

v3 whole, which is shorter than its diff:
```python
import jax
import jax.numpy as jnp
from jax import lax
from jax.experimental import pallas as pl
from jax.experimental.pallas import tpu as pltpu
from jax.sharding import PartitionSpec as P

learn_rate = 0.4
mean_rate = 0.25
MESH = pl.DeviceIdType.MESH
SIDE = 4
GROUP = 16
BLOCK = 128
f32 = jnp.float32
bf16 = jnp.bfloat16

FIRST = ("x", "y", "x", "y")
CHUNKS = ((0, 0, BLOCK), (1, 0, BLOCK), (2, 0, BLOCK), (3, 0, BLOCK))
PAIRS = ((0, 1), (2, 3))
DIRECT = (False, False, True, True)
FAR_FIRST = (8, 7, 9, 6, 10, 5, 11, 4, 12, 3, 13, 2, 14, 1, 15)


def row_sums(a):
    return jnp.sum(a.T, axis=0, keepdims=True)


def column_sums(a):
    return jnp.sum(a, axis=0, keepdims=True)


def along_rows(line):
    return jnp.broadcast_to(line, (BLOCK, line.shape[1])).T


def along_columns(line):
    return jnp.broadcast_to(line, (BLOCK, BLOCK))


SUMS = (row_sums, row_sums, row_sums, column_sums)
SPREAD = (along_rows, along_rows, along_rows, along_columns)


def kernel(
    gq, gk, gv, gm, gn, gb, wq, wk, wv, wm, wn, wb,
    whole, fresh, small_all, small_new,
    grad, first_in, total, second_in, weight,
    own_norms, slope_norms, small_grad, small_in, small_weight,
    load_sem, send_sem, recv_sem, norm_send, norm_recv, small_send, small_recv, small_load,
):
    b = lax.axis_index("batch")
    c = lax.axis_index("cols")
    y, x = b // SIDE, lax.rem(b, SIDE)
    place = {"y": y, "x": x}
    at = {(a, s): lax.rem(place[a] + s + SIDE, SIDE) for a in "yx" for s in (0, 1, -1, 2)}
    near = {(a, s): ((at[a, s] * SIDE + x) if a == "y" else (y * SIDE + at[a, s]), c) for a in "yx" for s in (1, -1, 2)}
    across = {k: lax.rem(c + k, GROUP) for k in range(1, GROUP)}

    barrier = pltpu.get_barrier_semaphore()
    for a in "yx":
        for s in (1, -1):
            pl.semaphore_signal(barrier, inc=1, device_id=near[a, s], device_id_type=MESH)
    for k in FAR_FIRST:
        pl.semaphore_signal(barrier, inc=1, device_id=(b, across[k]), device_id_type=MESH)

    loads = {}

    def quarter(t, j):
        return grad.at[t, :, j] if FIRST[t] == "x" else grad.at[t, j]

    def start_load(t, n, j):
        g = (gq, gk, gv, gm)[t]
        if t < 3:
            src = g.at[:, j] if FIRST[t] == "x" else g.at[j]
            copy = pltpu.make_async_copy(src, quarter(t, j), load_sem.at[t, n])
            copy.start()
        else:
            for i in range(SIDE):
                at_column = pl.multiple_of((j * SIDE + i) * BLOCK, BLOCK)
                pltpu.make_async_copy(
                    g.at[:, pl.ds(at_column, BLOCK)], grad.at[t, j, i], load_sem.at[t, n]
                ).start()
            copy = pltpu.make_async_copy(quarter(t, j), quarter(t, j), load_sem.at[t, n])
        loads[t, n] = copy

    steps = (2, 1, -1, 0)
    for pair in (0, 1):
        for n, step in enumerate(steps):
            for t in (2 * pair, 2 * pair + 1):
                start_load(t, n, at[FIRST[t], step])
        if pair == 0:
            weight_copies = []
            for t, w in enumerate((wq, wk, wv, wm)):
                copy = pltpu.make_async_copy(w, weight.at[t], load_sem.at[t, 4])
                copy.start()
                weight_copies.append(copy)
            small_copies = [
                pltpu.make_async_copy(gn, small_grad.at[0], small_load.at[0]),
                pltpu.make_async_copy(gb, small_grad.at[1], small_load.at[1]),
                pltpu.make_async_copy(wn, small_weight.at[pl.ds(0, 1)], small_load.at[2]),
                pltpu.make_async_copy(wb, small_weight.at[pl.ds(1, 1)], small_load.at[3]),
            ]
            for copy in small_copies:
                copy.start()

    pl.semaphore_wait(barrier, 4 + GROUP - 1)

    sent = []
    flight = {}

    def send(key, src, dst, device):
        n = len(sent)
        copy = pltpu.make_async_remote_copy(
            src_ref=src,
            dst_ref=dst,
            send_sem=send_sem.at[n],
            recv_sem=recv_sem.at[n],
            device_id=device,
            device_id_type=MESH,
        )
        copy.start()
        sent.append(copy)
        flight[key] = copy

    def receive(*key):
        flight.pop(key).wait_recv()

    def first(k):
        return FIRST[CHUNKS[k][0]]

    def second(k):
        return "y" if first(k) == "x" else "x"

    def rows(k, h=None):
        _, r, n = CHUNKS[k]
        return pl.ds(r, n) if h is None else pl.ds(r + h * n // 2, n // 2)

    def pick(k, j, h):
        t = CHUNKS[k][0]
        return (t, pl.ds(2 * h, 2), j, rows(k)) if first(k) == "x" else (t, j, pl.ds(2 * h, 2), rows(k))

    def landing(k, n):
        return (CHUNKS[k][0], n, slice(None), rows(k))

    def loaded(k, n):
        t = CHUNKS[k][0]
        if (t, n) in loads:
            loads.pop((t, n)).wait()

    def opened(k):
        a = first(k)
        up, down = near[a, 1], near[a, -1]
        loaded(k, 0)
        send((k, "far", 1), grad.at[pick(k, at[a, 2], 0)], first_in.at[landing(k, 0)], up)
        send((k, "far", -1), grad.at[pick(k, at[a, 2], 1)], first_in.at[landing(k, 1)], down)
        loaded(k, 1)
        send((k, "near", 1), grad.at[pick(k, at[a, 1], 1)], first_in.at[landing(k, 2)], up)
        loaded(k, 2)
        send((k, "near", -1), grad.at[pick(k, at[a, -1], 0)], first_in.at[landing(k, 3)], down)

    def relayed(k):
        a = first(k)
        receive(k, "far", 1)
        here = landing(k, 0)
        first_in[here] = first_in[here] + grad[pick(k, at[a, 1], 0)]
        send((k, "both", 1), first_in.at[here], first_in.at[landing(k, 4)], near[a, 1])
        receive(k, "far", -1)
        here = landing(k, 1)
        first_in[here] = first_in[here] + grad[pick(k, at[a, -1], 1)]
        send((k, "both", -1), first_in.at[here], first_in.at[landing(k, 5)], near[a, -1])

    def closed(k):
        t, a = CHUNKS[k][0], first(k)
        loaded(k, 3)
        receive(k, "near", -1)
        receive(k, "both", 1)
        total[t, pl.ds(0, 2), rows(k)] = (
            grad[pick(k, at[a, 0], 0)] + first_in[landing(k, 3)] + first_in[landing(k, 4)]
        )
        receive(k, "near", 1)
        receive(k, "both", -1)
        total[t, pl.ds(2, 2), rows(k)] = (
            grad[pick(k, at[a, 0], 1)] + first_in[landing(k, 2)] + first_in[landing(k, 5)]
        )
        a = second(k)
        for n, step in enumerate((2, 1, -1)):
            send((k, "sum", step), total.at[t, at[a, step], rows(k)], second_in.at[t, n, rows(k)], near[a, step])

    def summed(k):
        t, a = CHUNKS[k][0], second(k)
        for step in (1, -1, 2):
            receive(k, "sum", step)
        mean = total[t, at[a, 0], rows(k)] + second_in[t, 0, rows(k)]
        mean = (mean + (second_in[t, 1, rows(k)] + second_in[t, 2, rows(k)])) * mean_rate
        fresh[t, rows(k)] = mean
        return SUMS[t](mean * mean)

    def to_cols(buffer, n):
        for k in FAR_FIRST:
            pltpu.make_async_remote_copy(
                src_ref=buffer.at[c],
                dst_ref=buffer.at[c],
                send_sem=norm_send.at[n],
                recv_sem=norm_recv.at[n],
                device_id=(b, across[k]),
                device_id_type=MESH,
            ).start()

    def wait_fifteen(buffer, sem):
        part = buffer.at[pl.ds(0, GROUP - 1)]
        pltpu.make_async_copy(part, part, sem).wait()

    def norms(pair):
        for i, k in enumerate(PAIRS[pair]):
            line = summed(k)
            slope_norms[pair, c, pl.ds(i, 1), pl.ds(0, line.shape[1])] = line
        to_cols(slope_norms.at[pair], 1 + pair)

    def cell(k, j1, j2, h=None):
        t = CHUNKS[k][0]
        return whole.at[(t, j2, j1, rows(k, h)) if first(k) == "x" else (t, j1, j2, rows(k, h))]

    def spread(k, offset, direct):
        a = first(k)
        block = cell(k, at[a, 0], at[second(k), offset])
        for step in (2, 1, -1) if direct else (1, -1):
            send((k, "block", offset, step), block, block, near[a, step])

    def passed(k, offset):
        a = first(k)
        j2 = at[second(k), offset]
        receive(k, "block", offset, 1)
        half = cell(k, at[a, -1], j2, 0)
        send((k, "half", offset, 1), half, half, near[a, 1])
        receive(k, "block", offset, -1)
        half = cell(k, at[a, 1], j2, 1)
        send((k, "half", offset, -1), half, half, near[a, -1])

    def step(pair):
        wait_fifteen(slope_norms.at[pair], norm_recv.at[1 + pair])
        slopes = jnp.sum(slope_norms[pair], axis=0)
        for i, k in enumerate(PAIRS[pair]):
            t, r, n = CHUNKS[k]
            a = second(k)
            ratio = jnp.sqrt(own_sum[t : t + 1, r : r + n] if t < 3 else own_sum[t : t + 1]) * lax.rsqrt(
                slopes[i : i + 1, :n] + 1e-06
            )
            new = weight[t, rows(k)] - learn_rate * (fresh[t, rows(k)] * SPREAD[t](ratio))
            fresh[t, rows(k)] = new
            whole[t, y, x, rows(k)] = new.astype(bf16)
        for k in PAIRS[pair]:
            block = cell(k, at[first(k), 0], at[second(k), 0])
            for s in (2, 1, -1):
                send((k, "line", s), block, block, near[second(k), s])
            spread(k, 0, DIRECT[k])

    def lined(k):
        for s in (1, -1, 2):
            receive(k, "line", s)
            spread(k, -s if s != 2 else 2, DIRECT[k])

    def small_out():
        for copy in small_copies:
            copy.wait()
        for k in range(1, GROUP):
            peer = lax.rem(b + k, GROUP)
            at_lane = pl.multiple_of(peer * BLOCK, BLOCK)
            for i in (0, 1):
                pltpu.make_async_remote_copy(
                    src_ref=small_grad.at[i, :, pl.ds(at_lane, BLOCK)],
                    dst_ref=small_in.at[b, pl.ds(i, 1)],
                    send_sem=small_send.at[0],
                    recv_sem=small_recv.at[0],
                    device_id=(peer, c),
                    device_id_type=MESH,
                ).start()
        own_lane = pl.multiple_of(b * BLOCK, BLOCK)
        small_in[b, pl.ds(0, 1)] = small_grad[0, :, pl.ds(own_lane, BLOCK)]
        small_in[b, pl.ds(1, 1)] = small_grad[1, :, pl.ds(own_lane, BLOCK)]

    def small_step():
        wait_fifteen(small_in, small_recv.at[0])
        small_sum = small_in[0]
        for i in range(1, GROUP):
            small_sum = small_sum + small_in[i]
        small_step = small_weight[...] - learn_rate * (small_sum * mean_rate)
        small_new[...] = small_step
        small_all[b] = small_step
        for k in range(1, GROUP):
            pltpu.make_async_remote_copy(
                src_ref=small_new,
                dst_ref=small_all.at[b],
                send_sem=small_send.at[1],
                recv_sem=small_recv.at[1],
                device_id=(lax.rem(b + k, GROUP), c),
                device_id_type=MESH,
            ).start()

    opened(0)
    opened(1)
    opened(2)
    opened(3)
    for t in range(4):
        weight_copies[t].wait()
        own_norms[c, pl.ds(t, 1)] = SUMS[t](weight[t] * weight[t])
    to_cols(own_norms, 0)
    relayed(0)
    relayed(1)
    relayed(2)
    relayed(3)
    closed(0)
    closed(1)
    closed(2)
    closed(3)
    norms(0)
    norms(1)
    wait_fifteen(own_norms, norm_recv.at[0])
    own_sum = jnp.sum(own_norms[...], axis=0)
    small_out()
    step(0)
    step(1)
    passed(0, 0)
    passed(1, 0)
    lined(0)
    lined(1)
    small_step()
    lined(2)
    lined(3)
    for k in (0, 1):
        for offset in (-1, 1, 2):
            passed(k, offset)

    for copy in flight.values():
        copy.wait_recv()
    wait_fifteen(small_all, small_recv.at[1])
    for copy in sent:
        copy.wait_send()
    for n, buffer in ((0, own_norms), (1, slope_norms.at[0]), (2, slope_norms.at[1])):
        wait_fifteen(buffer, norm_send.at[n])
    wait_fifteen(small_in, small_send.at[0])
    wait_fifteen(small_all, small_send.at[1])


def write_out(whole, fresh, small_all, small_own, cq, ck, cv, cm, cn, cb, nq, nk, nv, nm, nn, nb, small, sem):
    copies = []

    def start(src, dst):
        copy = pltpu.make_async_copy(src, dst, sem.at[len(copies)])
        copy.start()
        copies.append(copy)

    for t, out in enumerate((cq, ck, cv)):
        start(whole.at[t], out)
    for j in range(GROUP):
        start(whole.at[3, j // SIDE, j % SIDE], cm.at[:, pl.ds(j * BLOCK, BLOCK)])
    for t, out in enumerate((nq, nk, nv, nm)):
        start(fresh.at[t], out)
    for i, out in enumerate((nn, nb)):
        start(small_own.at[pl.ds(i, 1)], out)
    for i, out in enumerate((cn, cb)):
        small[i] = small_all[:, i].astype(bf16)
        start(small.at[i], out)
    for copy in copies:
        copy.wait()


def per_device(gq, gk, gv, gm, gn, gb, wq, wk, wv, wm, wn, wb):
    blocks = (SIDE, SIDE, BLOCK, BLOCK)
    any_space = pl.BlockSpec(memory_space=pl.ANY)
    in_place = pl.BlockSpec(memory_space=pltpu.VMEM)
    shape = jax.ShapeDtypeStruct
    results = pl.pallas_call(
        kernel,
        out_shape=(
            pltpu.VMEM((4, *blocks), bf16),
            pltpu.VMEM((4, BLOCK, BLOCK), f32),
            pltpu.VMEM((GROUP, 2, BLOCK), f32),
            pltpu.VMEM((2, BLOCK), f32),
        ),
        in_specs=[any_space] * 12,
        out_specs=(in_place,) * 4,
        scratch_shapes=[
            pltpu.VMEM((4, *blocks), f32),
            pltpu.VMEM((4, 6, 2, BLOCK, BLOCK), f32),
            pltpu.VMEM((4, SIDE, BLOCK, BLOCK), f32),
            pltpu.VMEM((4, 3, BLOCK, BLOCK), f32),
            pltpu.VMEM((4, BLOCK, BLOCK), f32),
            pltpu.VMEM((GROUP, 4, BLOCK), f32),
            pltpu.VMEM((2, GROUP, 2, BLOCK), f32),
            pltpu.VMEM((2, 1, GROUP * BLOCK), f32),
            pltpu.VMEM((GROUP, 2, BLOCK), f32),
            pltpu.VMEM((2, BLOCK), f32),
            pltpu.SemaphoreType.DMA((4, 5)),
            pltpu.SemaphoreType.DMA((120,)),
            pltpu.SemaphoreType.DMA((120,)),
            pltpu.SemaphoreType.DMA((3,)),
            pltpu.SemaphoreType.DMA((3,)),
            pltpu.SemaphoreType.DMA((2,)),
            pltpu.SemaphoreType.DMA((2,)),
            pltpu.SemaphoreType.DMA((4,)),
        ],
        compiler_params=pltpu.CompilerParams(
            collective_id=0, has_side_effects=True, vmem_limit_bytes=24 * 1024 * 1024
        ),
        name="step",
    )(*(
        pltpu.with_memory_space_constraint(a, pltpu.HBM)
        for a in (
            gq.reshape(blocks), gk.reshape(blocks), gv.reshape(blocks), gm[0], gn, gb,
            wq, wk, wv, wm, wn.reshape(1, BLOCK), wb.reshape(1, BLOCK),
        )
    ))
    cq, ck, cv, cm, cn, cb, nq, nk, nv, nm, nn, nb = pl.pallas_call(
        write_out,
        out_shape=(
            shape(blocks, bf16), shape(blocks, bf16), shape(blocks, bf16), shape((BLOCK, GROUP * BLOCK), bf16),
            shape((GROUP, BLOCK), bf16), shape((GROUP, BLOCK), bf16),
            shape((BLOCK, BLOCK), f32), shape((BLOCK, BLOCK), f32), shape((BLOCK, BLOCK), f32), shape((BLOCK, BLOCK), f32),
            shape((1, BLOCK), f32), shape((1, BLOCK), f32),
        ),
        in_specs=[in_place] * 4,
        out_specs=(any_space,) * 12,
        scratch_shapes=[pltpu.VMEM((2, GROUP, BLOCK), bf16), pltpu.SemaphoreType.DMA((32,))],
        compiler_params=pltpu.CompilerParams(vmem_limit_bytes=8 * 1024 * 1024),
        name="write_out",
    )(*(pltpu.with_memory_space_constraint(a, pltpu.VMEM) for a in results))
    whole = (GROUP * BLOCK, BLOCK)
    return (
        cq.reshape(whole), ck.reshape(whole), cv.reshape(whole), cm,
        cn.reshape(-1), cb.reshape(-1),
        nq, nk, nv, nm, nn.reshape(-1), nb.reshape(-1),
    )


def solution(mesh):
    cut = P("batch", "cols")
    in_specs = (
        P("batch", None, "cols"), P("batch", None, "cols"), P("batch", None, "cols"), P("batch", "cols", None),
        P("batch", None), P("batch", None), cut, cut, cut, P("cols", "batch"), P("batch"), P("batch"),
    )
    out_specs = (
        P(None, "cols"), P(None, "cols"), P(None, "cols"), P("cols", None), P(), P(),
        cut, cut, cut, P("cols", "batch"), P("batch"), P("batch"),
    )
    return jax.shard_map(per_device, mesh=mesh, in_specs=in_specs, out_specs=out_specs, check_vma=False)
```

time: 65.3 us -> 58.9 us (0.902)
  the two profiles are of different devices: /device:TPU:32 before, /device:TPU:1 now
where the time goes in v3:
time: 58.9 us; the launch traced here: 58.8 us
  Pallas kernels  58.1 us (99%)
  between operations  0.66 us (1%)
    pallas_call x1, Pallas kernels, per_device(): pl.pallas_call(kernel, out_shape=(pltpu.VMEM((4, *blocks), bf16), pltpu.V...  56.5 us
    pallas_call x1, Pallas kernels, per_device(): pl.pallas_call(write_out, out_shape=(shape(blocks, bf16), shape(blocks, b...  1.68 us

profile of v3, /device:TPU:1, one launch (start us, length us, event | category | flops | bytes accessed | tf_op | source)
XLA Modules:
  0.0 58.8 jit_solution(17329255239175770339)
XLA Ops:
  0.6 56.5 %step.1 = (bf16[4,4,4,128,128]{4,3,2,1,0:T(8,128)(2,1)S(1)}, f32[4,128,128]{2,1,0:T(8,128)S(1)}, f32[16,2,128]{2,1,0:T(2,128)S(1)}, f32[2,128]{1,0:T(2,128)S(1)}) custom-call(f32[4,4,128,128]{3,2,1,0:T(8,128)} %bitcast.13, f32[4,4,128,128]{3,2,1,0:T(8,128)} %bitcast.14, f32[4,4,128,128]{3,2,1,0:T(8,128)} %bitcast.15, f32[128,2048]{1,0:T(8,128)} %bitcast.16, ...), custom_call_target="tpu_custom_call" | custom-call | tf_op jit(solution)/shard_map/step/pallas_call | solution.py:372
  57.1 1.7 %write_out.1 = (bf16[4,4,128,128]{3,2,1,0:T(8,128)(2,1)}, bf16[4,4,128,128]{3,2,1,0:T(8,128)(2,1)}, bf16[4,4,128,128]{3,2,1,0:T(8,128)(2,1)}, bf16[128,2048]{1,0...) custom-call(bf16[4,4,4,128,128]{4,3,2,1,0:T(8,128)(2,1)S(1)} %get-tu, ...), custom_call_target="tpu_custom_call" | custom-call | tf_op jit(solution)/shard_map/write_out/pallas_call | solution.py:413

commit v4 on v3

--- a/solution.py
+++ b/solution.py
@@ -11,13 +11,14 @@
 SIDE = 4
 GROUP = 16
 BLOCK = 128
+HALF = 64
 f32 = jnp.float32
 bf16 = jnp.bfloat16
 
 FIRST = ("x", "y", "x", "y")
 CHUNKS = ((0, 0, BLOCK), (1, 0, BLOCK), (2, 0, BLOCK), (3, 0, BLOCK))
 PAIRS = ((0, 1), (2, 3))
-DIRECT = (False, False, True, True)
+DIRECT = (False, False, False, False)
 FAR_FIRST = (8, 7, 9, 6, 10, 5, 11, 4, 12, 3, 13, 2, 14, 1, 15)
 
 
@@ -39,12 +40,57 @@
 
 SUMS = (row_sums, row_sums, row_sums, column_sums)
 SPREAD = (along_rows, along_rows, along_rows, along_columns)
+
+
+FIRST_STEPS = 118 * 256.0
+SECOND_STEPS = 127 * 256.0
+SLAB = 32
+
+
+def rounded(a):
+    head = a.astype(bf16)
+    wide = head.astype(f32)
+    return head, (a - wide) / jnp.maximum(jnp.abs(wide), 1e-30)
+
+
+def encode(a, b):
+    head_a, left_a = rounded(a)
+    head_b, left_b = rounded(b)
+    power = jnp.round(left_a * FIRST_STEPS)
+    level = jnp.round(left_b * SECOND_STEPS)
+    rest = jnp.where(level < 0, level - 128.0, level + 128.0) * jnp.exp2(power)
+    return head_a, head_b, rest.astype(bf16)
+
+
+def decode(head_a, head_b, rest):
+    a, b, rest = head_a.astype(f32), head_b.astype(f32), rest.astype(f32)
+    size = jnp.abs(rest)
+    power = jnp.floor(jnp.log(size) * 1.4426950408889634 + 0.002) - 7.0
+    level = size * jnp.exp2(-power) - 128.0
+    level = jnp.where(rest < 0, -level, level)
+    return a + jnp.abs(a) * (power * (1 / FIRST_STEPS)), b + jnp.abs(b) * (level * (1 / SECOND_STEPS))
+
+
+def slabs(rows, body):
+    def one(i, carry):
+        body(pl.ds(pl.multiple_of(i * SLAB, SLAB), SLAB))
+        return carry
+
+    lax.fori_loop(0, rows // SLAB, one, 0)
+
+
+def put(ref, at, r, a, b):
+    ref[(*at, 0, r)], ref[(*at, 1, r)], ref[(*at, 2, r)] = encode(a, b)
+
+
+def get(ref, at, r):
+    return decode(ref[(*at, 0, r)], ref[(*at, 1, r)], ref[(*at, 2, r)])
 
 
 def kernel(
     gq, gk, gv, gm, gn, gb, wq, wk, wv, wm, wn, wb,
     whole, fresh, small_all, small_new,
-    grad, first_in, total, second_in, weight,
+    grad, first_out, first_in, total, second_out, second_in, weight,
     own_norms, slope_norms, small_grad, small_in, small_weight,
     load_sem, send_sem, recv_sem, norm_send, norm_recv, small_send, small_recv, small_load,
 ):
@@ -83,25 +129,19 @@
             copy = pltpu.make_async_copy(quarter(t, j), quarter(t, j), load_sem.at[t, n])
         loads[t, n] = copy
 
-    steps = (2, 1, -1, 0)
-    for pair in (0, 1):
-        for n, step in enumerate(steps):
+    def start_loads(pair):
+        for n, step in enumerate((2, 1, -1, 0)):
             for t in (2 * pair, 2 * pair + 1):
                 start_load(t, n, at[FIRST[t], step])
-        if pair == 0:
-            weight_copies = []
-            for t, w in enumerate((wq, wk, wv, wm)):
-                copy = pltpu.make_async_copy(w, weight.at[t], load_sem.at[t, 4])
-                copy.start()
-                weight_copies.append(copy)
-            small_copies = [
-                pltpu.make_async_copy(gn, small_grad.at[0], small_load.at[0]),
-                pltpu.make_async_copy(gb, small_grad.at[1], small_load.at[1]),
-                pltpu.make_async_copy(wn, small_weight.at[pl.ds(0, 1)], small_load.at[2]),
-                pltpu.make_async_copy(wb, small_weight.at[pl.ds(1, 1)], small_load.at[3]),
-            ]
-            for copy in small_copies:
-                copy.start()
+
+    weight_copies = [pltpu.make_async_copy(w, weight.at[t], load_sem.at[t, 4]) for t, w in enumerate((wq, wk, wv, wm))]
+    small_copies = [
+        pltpu.make_async_copy(gn, small_grad.at[0], small_load.at[0]),
+        pltpu.make_async_copy(gb, small_grad.at[1], small_load.at[1]),
+        pltpu.make_async_copy(wn, small_weight.at[pl.ds(0, 1)], small_load.at[2]),
+        pltpu.make_async_copy(wb, small_weight.at[pl.ds(1, 1)], small_load.at[3]),
+    ]
+    start_loads(0)
 
     pl.semaphore_wait(barrier, 4 + GROUP - 1)
 
@@ -135,65 +175,82 @@
         _, r, n = CHUNKS[k]
         return pl.ds(r, n) if h is None else pl.ds(r + h * n // 2, n // 2)
 
-    def pick(k, j, h):
-        t = CHUNKS[k][0]
-        return (t, pl.ds(2 * h, 2), j, rows(k)) if first(k) == "x" else (t, j, pl.ds(2 * h, 2), rows(k))
-
-    def landing(k, n):
-        return (CHUNKS[k][0], n, slice(None), rows(k))
+    def pair_of(k, j, h, r):
+        if first(k) == "x":
+            return grad[k, 2 * h, j, r], grad[k, 2 * h + 1, j, r]
+        return grad[k, j, 2 * h, r], grad[k, j, 2 * h + 1, r]
 
     def loaded(k, n):
-        t = CHUNKS[k][0]
-        if (t, n) in loads:
-            loads.pop((t, n)).wait()
+        if (k, n) in loads:
+            loads.pop((k, n)).wait()
+
+    def send_first(k, name, n, step):
+        send((k, name, step), first_out.at[k, n], first_in.at[k, n], near[first(k), step])
+
+    def open_half(k, name, n, step, j, h):
+        slabs(BLOCK, lambda r: put(first_out, (k, n), r, *pair_of(k, j, h, r)))
+        send_first(k, name, n, step)
 
     def opened(k):
-        a = first(k)
-        up, down = near[a, 1], near[a, -1]
         loaded(k, 0)
-        send((k, "far", 1), grad.at[pick(k, at[a, 2], 0)], first_in.at[landing(k, 0)], up)
-        send((k, "far", -1), grad.at[pick(k, at[a, 2], 1)], first_in.at[landing(k, 1)], down)
+        open_half(k, "far", 0, 1, at[first(k), 2], 0)
+        open_half(k, "far", 1, -1, at[first(k), 2], 1)
+
+    def opened_near(k):
         loaded(k, 1)
-        send((k, "near", 1), grad.at[pick(k, at[a, 1], 1)], first_in.at[landing(k, 2)], up)
+        open_half(k, "near", 2, 1, at[first(k), 1], 1)
         loaded(k, 2)
-        send((k, "near", -1), grad.at[pick(k, at[a, -1], 0)], first_in.at[landing(k, 3)], down)
+        open_half(k, "near", 3, -1, at[first(k), -1], 0)
 
     def relayed(k):
-        a = first(k)
-        receive(k, "far", 1)
-        here = landing(k, 0)
-        first_in[here] = first_in[here] + grad[pick(k, at[a, 1], 0)]
-        send((k, "both", 1), first_in.at[here], first_in.at[landing(k, 4)], near[a, 1])
-        receive(k, "far", -1)
-        here = landing(k, 1)
-        first_in[here] = first_in[here] + grad[pick(k, at[a, -1], 1)]
-        send((k, "both", -1), first_in.at[here], first_in.at[landing(k, 5)], near[a, -1])
+        for h, step in ((0, 1), (1, -1)):
+            receive(k, "far", step)
+
+            def add(r):
+                a, b = get(first_in, (k, h), r)
+                own_a, own_b = pair_of(k, at[first(k), step], h, r)
+                put(first_out, (k, 4 + h), r, a + own_a, b + own_b)
+
+            slabs(BLOCK, add)
+            send_first(k, "both", 4 + h, step)
 
     def closed(k):
-        t, a = CHUNKS[k][0], first(k)
         loaded(k, 3)
-        receive(k, "near", -1)
-        receive(k, "both", 1)
-        total[t, pl.ds(0, 2), rows(k)] = (
-            grad[pick(k, at[a, 0], 0)] + first_in[landing(k, 3)] + first_in[landing(k, 4)]
-        )
-        receive(k, "near", 1)
-        receive(k, "both", -1)
-        total[t, pl.ds(2, 2), rows(k)] = (
-            grad[pick(k, at[a, 0], 1)] + first_in[landing(k, 2)] + first_in[landing(k, 5)]
-        )
-        a = second(k)
+        for h, step in ((0, 1), (1, -1)):
+            receive(k, "near", -step)
+            receive(k, "both", step)
+
+            def add(r):
+                a, b = pair_of(k, at[first(k), 0], h, r)
+                near_a, near_b = get(first_in, (k, 3 - h), r)
+                both_a, both_b = get(first_in, (k, 4 + h), r)
+                total[k, 2 * h, r] = a + near_a + both_a
+                total[k, 2 * h + 1, r] = b + near_b + both_b
+
+            slabs(BLOCK, add)
         for n, step in enumerate((2, 1, -1)):
-            send((k, "sum", step), total.at[t, at[a, step], rows(k)], second_in.at[t, n, rows(k)], near[a, step])
+            j = at[second(k), step]
+            slabs(HALF, lambda r: put(second_out, (k, n), r, total[k, j, r], total[k, j, lower(r)]))
+            send((k, "sum", step), second_out.at[k, n], second_in.at[k, n], near[second(k), step])
+
+    def lower(r):
+        return pl.ds(pl.multiple_of(r.start + HALF, SLAB), SLAB)
 
     def summed(k):
-        t, a = CHUNKS[k][0], second(k)
         for step in (1, -1, 2):
             receive(k, "sum", step)
-        mean = total[t, at[a, 0], rows(k)] + second_in[t, 0, rows(k)]
-        mean = (mean + (second_in[t, 1, rows(k)] + second_in[t, 2, rows(k)])) * mean_rate
-        fresh[t, rows(k)] = mean
-        return SUMS[t](mean * mean)
+
+        def add(r):
+            top, bottom = total[k, at[second(k), 0], r], total[k, at[second(k), 0], lower(r)]
+            for n in range(3):
+                a, b = get(second_in, (k, n), r)
+                top, bottom = top + a, bottom + b
+            fresh[k, r] = top * mean_rate
+            fresh[k, lower(r)] = bottom * mean_rate
+
+        slabs(HALF, add)
+        mean = fresh[k]
+        return SUMS[k](mean * mean)
 
     def to_cols(buffer, n):
         for k in FAR_FIRST:
@@ -298,8 +355,15 @@
 
     opened(0)
     opened(1)
+    opened_near(0)
+    opened_near(1)
+    start_loads(1)
+    for copy in weight_copies + small_copies:
+        copy.start()
     opened(2)
     opened(3)
+    opened_near(2)
+    opened_near(3)
     for t in range(4):
         weight_copies[t].wait()
         own_norms[c, pl.ds(t, 1)] = SUMS[t](weight[t] * weight[t])
@@ -323,10 +387,12 @@
     passed(1, 0)
     lined(0)
     lined(1)
+    passed(2, 0)
+    passed(3, 0)
     small_step()
     lined(2)
     lined(3)
-    for k in (0, 1):
+    for k in (0, 1, 2, 3):
         for offset in (-1, 1, 2):
             passed(k, offset)
 
@@ -381,9 +447,11 @@
         out_specs=(in_place,) * 4,
         scratch_shapes=[
             pltpu.VMEM((4, *blocks), f32),
-            pltpu.VMEM((4, 6, 2, BLOCK, BLOCK), f32),
+            pltpu.VMEM((4, 6, 3, BLOCK, BLOCK), bf16),
+            pltpu.VMEM((4, 6, 3, BLOCK, BLOCK), bf16),
             pltpu.VMEM((4, SIDE, BLOCK, BLOCK), f32),
-            pltpu.VMEM((4, 3, BLOCK, BLOCK), f32),
+            pltpu.VMEM((4, 3, 3, HALF, BLOCK), bf16),
+            pltpu.VMEM((4, 3, 3, HALF, BLOCK), bf16),
             pltpu.VMEM((4, BLOCK, BLOCK), f32),
             pltpu.VMEM((GROUP, 4, BLOCK), f32),
             pltpu.VMEM((2, GROUP, 2, BLOCK), f32),

time: 58.9 us -> 53.9 us (0.915)
  the two profiles are of different devices: /device:TPU:1 before, /device:TPU:32 now
where the time goes in v4:
time: 53.9 us; the launch traced here: 53.5 us
  Pallas kernels  52.8 us (98%)
  between operations  0.66 us (1%)
    pallas_call x1, Pallas kernels, per_device(): pl.pallas_call(kernel, out_shape=(pltpu.VMEM((4, *blocks), bf16), pltpu.V...  51.2 us
    pallas_call x1, Pallas kernels, per_device(): pl.pallas_call(write_out, out_shape=(shape(blocks, bf16), shape(blocks, b...  1.68 us

profile of v4, /device:TPU:32, one launch (start us, length us, event | category | flops | bytes accessed | tf_op | source)
XLA Modules:
  0.0 53.5 jit_solution(12178472300947184360)
XLA Ops:
  0.6 51.2 %step.1 = (bf16[4,4,4,128,128]{4,3,2,1,0:T(8,128)(2,1)S(1)}, f32[4,128,128]{2,1,0:T(8,128)S(1)}, f32[16,2,128]{2,1,0:T(2,128)S(1)}, f32[2,128]{1,0:T(2,128)S(1)}) custom-call(f32[4,4,128,128]{3,2,1,0:T(8,128)} %bitcast.13, f32[4,4,128,128]{3,2,1,0:T(8,128)} %bitcast.14, f32[4,4,128,128]{3,2,1,0:T(8,128)} %bitcast.15, f32[128,2048]{1,0:T(8,128)} %bitcast.16, ...), custom_call_target="tpu_custom_call" | custom-call | tf_op jit(solution)/shard_map/step/pallas_call | solution.py:438
  51.8 1.7 %write_out.1 = (bf16[4,4,128,128]{3,2,1,0:T(8,128)(2,1)}, bf16[4,4,128,128]{3,2,1,0:T(8,128)(2,1)}, bf16[4,4,128,128]{3,2,1,0:T(8,128)(2,1)}, bf16[128,2048]{1,0...) custom-call(bf16[4,4,4,128,128]{4,3,2,1,0:T(8,128)(2,1)S(1)} %get-tu, ...), custom_call_target="tpu_custom_call" | custom-call | tf_op jit(solution)/shard_map/write_out/pallas_call | solution.py:481

commit v5 on v4

--- a/solution.py
+++ b/solution.py
@@ -16,9 +16,12 @@
 bf16 = jnp.bfloat16
 
 FIRST = ("x", "y", "x", "y")
-CHUNKS = ((0, 0, BLOCK), (1, 0, BLOCK), (2, 0, BLOCK), (3, 0, BLOCK))
-PAIRS = ((0, 1), (2, 3))
-DIRECT = (False, False, False, False)
+CHUNKS = ((0, 0, 128), (1, 0, 128), (2, 0, 128), (3, 0, 128))
+GROUPS = ((0, 1), (2, 3))
+ORDER = """
+oF1 oF2 oF3 oF0 oN2 oN1 oN3 re2 oN0 re3 re0 re1 cl2 cl3 cl1 cl0 su1 su0 st1 st0 l12 l22 l23 l13
+l10 p00 l21 l11 p23 l20 p22 p03 p01 p13 p12 p02 p10 p21 p11 p20
+""".split()
 FAR_FIRST = (8, 7, 9, 6, 10, 5, 11, 4, 12, 3, 13, 2, 14, 1, 15)
 
 
@@ -69,22 +72,6 @@
     level = size * jnp.exp2(-power) - 128.0
     level = jnp.where(rest < 0, -level, level)
     return a + jnp.abs(a) * (power * (1 / FIRST_STEPS)), b + jnp.abs(b) * (level * (1 / SECOND_STEPS))
-
-
-def slabs(rows, body):
-    def one(i, carry):
-        body(pl.ds(pl.multiple_of(i * SLAB, SLAB), SLAB))
-        return carry
-
-    lax.fori_loop(0, rows // SLAB, one, 0)
-
-
-def put(ref, at, r, a, b):
-    ref[(*at, 0, r)], ref[(*at, 1, r)], ref[(*at, 2, r)] = encode(a, b)
-
-
-def get(ref, at, r):
-    return decode(ref[(*at, 0, r)], ref[(*at, 1, r)], ref[(*at, 2, r)])
 
 
 def kernel(
@@ -129,9 +116,9 @@
             copy = pltpu.make_async_copy(quarter(t, j), quarter(t, j), load_sem.at[t, n])
         loads[t, n] = copy
 
-    def start_loads(pair):
+    def start_loads(tensors):
         for n, step in enumerate((2, 1, -1, 0)):
-            for t in (2 * pair, 2 * pair + 1):
+            for t in tensors:
                 start_load(t, n, at[FIRST[t], step])
 
     weight_copies = [pltpu.make_async_copy(w, weight.at[t], load_sem.at[t, 4]) for t, w in enumerate((wq, wk, wv, wm))]
@@ -141,7 +128,11 @@
         pltpu.make_async_copy(wn, small_weight.at[pl.ds(0, 1)], small_load.at[2]),
         pltpu.make_async_copy(wb, small_weight.at[pl.ds(1, 1)], small_load.at[3]),
     ]
-    start_loads(0)
+    needed = []
+    for o in ORDER:
+        if CHUNKS[int(o[2])][0] not in needed and o[0] == "o":
+            needed.append(CHUNKS[int(o[2])][0])
+    start_loads(needed[:2])
 
     pl.semaphore_wait(barrier, 4 + GROUP - 1)
 
@@ -175,20 +166,41 @@
         _, r, n = CHUNKS[k]
         return pl.ds(r, n) if h is None else pl.ds(r + h * n // 2, n // 2)
 
+    def slabs(start, count, body):
+        def one(i, carry):
+            body(pl.multiple_of(start + i * SLAB, SLAB))
+            return carry
+
+        lax.fori_loop(0, count // SLAB, one, 0)
+
+    def cut(r):
+        return pl.ds(r, SLAB)
+
     def pair_of(k, j, h, r):
+        t = CHUNKS[k][0]
         if first(k) == "x":
-            return grad[k, 2 * h, j, r], grad[k, 2 * h + 1, j, r]
-        return grad[k, j, 2 * h, r], grad[k, j, 2 * h + 1, r]
+            return grad[t, 2 * h, j, cut(r)], grad[t, 2 * h + 1, j, cut(r)]
+        return grad[t, j, 2 * h, cut(r)], grad[t, j, 2 * h + 1, cut(r)]
+
+    def put(ref, r, values):
+        ref[0, cut(r)], ref[1, cut(r)], ref[2, cut(r)] = encode(*values)
+
+    def get(ref, r):
+        return decode(ref[0, cut(r)], ref[1, cut(r)], ref[2, cut(r)])
 
     def loaded(k, n):
-        if (k, n) in loads:
-            loads.pop((k, n)).wait()
+        t = CHUNKS[k][0]
+        if (t, n) in loads:
+            loads.pop((t, n)).wait()
 
     def send_first(k, name, n, step):
-        send((k, name, step), first_out.at[k, n], first_in.at[k, n], near[first(k), step])
+        t = CHUNKS[k][0]
+        src, dst = first_out.at[t, n, :, rows(k)], first_in.at[t, n, :, rows(k)]
+        send((k, name, step), src, dst, near[first(k), step])
 
     def open_half(k, name, n, step, j, h):
-        slabs(BLOCK, lambda r: put(first_out, (k, n), r, *pair_of(k, j, h, r)))
+        t, r0, count = CHUNKS[k]
+        slabs(r0, count, lambda r: put(first_out.at[t, n], r, pair_of(k, j, h, r)))
         send_first(k, name, n, step)
 
     def opened(k):
@@ -203,18 +215,21 @@
         open_half(k, "near", 3, -1, at[first(k), -1], 0)
 
     def relayed(k):
+        t, r0, count = CHUNKS[k]
         for h, step in ((0, 1), (1, -1)):
             receive(k, "far", step)
 
             def add(r):
-                a, b = get(first_in, (k, h), r)
+                a, b = get(first_in.at[t, h], r)
                 own_a, own_b = pair_of(k, at[first(k), step], h, r)
-                put(first_out, (k, 4 + h), r, a + own_a, b + own_b)
-
-            slabs(BLOCK, add)
+                put(first_out.at[t, 4 + h], r, (a + own_a, b + own_b))
+
+            loaded(k, 1 + h)
+            slabs(r0, count, add)
             send_first(k, "both", 4 + h, step)
 
     def closed(k):
+        t, r0, count = CHUNKS[k]
         loaded(k, 3)
         for h, step in ((0, 1), (1, -1)):
             receive(k, "near", -step)
@@ -222,35 +237,42 @@
 
             def add(r):
                 a, b = pair_of(k, at[first(k), 0], h, r)
-                near_a, near_b = get(first_in, (k, 3 - h), r)
-                both_a, both_b = get(first_in, (k, 4 + h), r)
-                total[k, 2 * h, r] = a + near_a + both_a
-                total[k, 2 * h + 1, r] = b + near_b + both_b
-
-            slabs(BLOCK, add)
+                near_a, near_b = get(first_in.at[t, 3 - h], r)
+                both_a, both_b = get(first_in.at[t, 4 + h], r)
+                total[t, 2 * h, cut(r)] = a + near_a + both_a
+                total[t, 2 * h + 1, cut(r)] = b + near_b + both_b
+
+            slabs(r0, count, add)
         for n, step in enumerate((2, 1, -1)):
             j = at[second(k), step]
-            slabs(HALF, lambda r: put(second_out, (k, n), r, total[k, j, r], total[k, j, lower(r)]))
-            send((k, "sum", step), second_out.at[k, n], second_in.at[k, n], near[second(k), step])
-
-    def lower(r):
-        return pl.ds(pl.multiple_of(r.start + HALF, SLAB), SLAB)
+
+            def halves(i):
+                r = pl.multiple_of(i + r0 // 2, SLAB)
+                low = pl.multiple_of(r + count // 2, SLAB)
+                put(second_out.at[t, n], i, (total[t, j, cut(r)], total[t, j, cut(low)]))
+
+            slabs(r0 // 2, count // 2, halves)
+            part = pl.ds(r0 // 2, count // 2)
+            send((k, "sum", step), second_out.at[t, n, :, part], second_in.at[t, n, :, part], near[second(k), step])
 
     def summed(k):
+        t, r0, count = CHUNKS[k]
         for step in (1, -1, 2):
             receive(k, "sum", step)
 
-        def add(r):
-            top, bottom = total[k, at[second(k), 0], r], total[k, at[second(k), 0], lower(r)]
+        def add(i):
+            r = pl.multiple_of(i + r0 // 2, SLAB)
+            low = pl.multiple_of(r + count // 2, SLAB)
+            top, bottom = total[t, at[second(k), 0], cut(r)], total[t, at[second(k), 0], cut(low)]
             for n in range(3):
-                a, b = get(second_in, (k, n), r)
+                a, b = get(second_in.at[t, n], i)
                 top, bottom = top + a, bottom + b
-            fresh[k, r] = top * mean_rate
-            fresh[k, lower(r)] = bottom * mean_rate
-
-        slabs(HALF, add)
-        mean = fresh[k]
-        return SUMS[k](mean * mean)
+            fresh[t, cut(r)] = top * mean_rate
+            fresh[t, cut(low)] = bottom * mean_rate
+
+        slabs(r0 // 2, count // 2, add)
+        mean = fresh[t, rows(k)]
+        return SUMS[t](mean * mean)
 
     def to_cols(buffer, n):
         for k in FAR_FIRST:
@@ -267,20 +289,20 @@
         part = buffer.at[pl.ds(0, GROUP - 1)]
         pltpu.make_async_copy(part, part, sem).wait()
 
-    def norms(pair):
-        for i, k in enumerate(PAIRS[pair]):
+    def norms(g):
+        for i, k in enumerate(GROUPS[g]):
             line = summed(k)
-            slope_norms[pair, c, pl.ds(i, 1), pl.ds(0, line.shape[1])] = line
-        to_cols(slope_norms.at[pair], 1 + pair)
+            slope_norms[g, c, pl.ds(i, 1), pl.ds(0, line.shape[1])] = line
+        to_cols(slope_norms.at[g], 1 + g)
 
     def cell(k, j1, j2, h=None):
         t = CHUNKS[k][0]
         return whole.at[(t, j2, j1, rows(k, h)) if first(k) == "x" else (t, j1, j2, rows(k, h))]
 
-    def spread(k, offset, direct):
+    def spread(k, offset):
         a = first(k)
         block = cell(k, at[a, 0], at[second(k), offset])
-        for step in (2, 1, -1) if direct else (1, -1):
+        for step in (1, -1):
             send((k, "block", offset, step), block, block, near[a, step])
 
     def passed(k, offset):
@@ -293,28 +315,27 @@
         half = cell(k, at[a, 1], j2, 1)
         send((k, "half", offset, -1), half, half, near[a, -1])
 
-    def step(pair):
-        wait_fifteen(slope_norms.at[pair], norm_recv.at[1 + pair])
-        slopes = jnp.sum(slope_norms[pair], axis=0)
-        for i, k in enumerate(PAIRS[pair]):
+    def step(g):
+        wait_fifteen(slope_norms.at[g], norm_recv.at[1 + g])
+        slopes = jnp.sum(slope_norms[g], axis=0)
+        for i, k in enumerate(GROUPS[g]):
             t, r, n = CHUNKS[k]
-            a = second(k)
-            ratio = jnp.sqrt(own_sum[t : t + 1, r : r + n] if t < 3 else own_sum[t : t + 1]) * lax.rsqrt(
-                slopes[i : i + 1, :n] + 1e-06
-            )
+            own = jnp.sum(own_norms[...], axis=0)[t : t + 1]
+            if t < 3:
+                own = own[:, r : r + n]
+            ratio = jnp.sqrt(own) * lax.rsqrt(slopes[i : i + 1, : own.shape[1]] + 1e-06)
             new = weight[t, rows(k)] - learn_rate * (fresh[t, rows(k)] * SPREAD[t](ratio))
             fresh[t, rows(k)] = new
             whole[t, y, x, rows(k)] = new.astype(bf16)
-        for k in PAIRS[pair]:
             block = cell(k, at[first(k), 0], at[second(k), 0])
             for s in (2, 1, -1):
                 send((k, "line", s), block, block, near[second(k), s])
-            spread(k, 0, DIRECT[k])
-
-    def lined(k):
-        for s in (1, -1, 2):
+            spread(k, 0)
+
+    def lined(k, *steps):
+        for s in steps:
             receive(k, "line", s)
-            spread(k, -s if s != 2 else 2, DIRECT[k])
+            spread(k, -s if s != 2 else 2)
 
     def small_out():
         for copy in small_copies:
@@ -353,55 +374,47 @@
                 device_id_type=MESH,
             ).start()
 
-    opened(0)
-    opened(1)
-    opened_near(0)
-    opened_near(1)
-    start_loads(1)
-    for copy in weight_copies + small_copies:
-        copy.start()
-    opened(2)
-    opened(3)
-    opened_near(2)
-    opened_near(3)
-    for t in range(4):
-        weight_copies[t].wait()
-        own_norms[c, pl.ds(t, 1)] = SUMS[t](weight[t] * weight[t])
-    to_cols(own_norms, 0)
-    relayed(0)
-    relayed(1)
-    relayed(2)
-    relayed(3)
-    closed(0)
-    closed(1)
-    closed(2)
-    closed(3)
-    norms(0)
-    norms(1)
-    wait_fifteen(own_norms, norm_recv.at[0])
-    own_sum = jnp.sum(own_norms[...], axis=0)
-    small_out()
-    step(0)
-    step(1)
-    passed(0, 0)
-    passed(1, 0)
-    lined(0)
-    lined(1)
-    passed(2, 0)
-    passed(3, 0)
-    small_step()
-    lined(2)
-    lined(3)
-    for k in (0, 1, 2, 3):
-        for offset in (-1, 1, 2):
-            passed(k, offset)
+    def own_out():
+        for t in range(4):
+            weight_copies[t].wait()
+            own_norms[c, pl.ds(t, 1)] = SUMS[t](weight[t] * weight[t])
+        to_cols(own_norms, 0)
+
+    run = {
+        "oF": opened,
+        "oN": opened_near,
+        "re": relayed,
+        "cl": closed,
+        "su": norms,
+        "st": step,
+        "p0": lambda k: passed(k, 0),
+        "l1": lambda k: lined(k, 1, -1),
+        "l2": lambda k: lined(k, 2),
+        "p1": lambda k: (passed(k, -1), passed(k, 1)),
+        "p2": lambda k: passed(k, 2),
+    }
+    seen = []
+    for o in ORDER:
+        if o[:2] == "re" and "re" not in seen:
+            own_out()
+        if o[:2] == "st" and "st" not in seen:
+            small_out()
+            wait_fifteen(own_norms, norm_recv.at[0])
+        if o[:2] == "p1" and "p1" not in seen:
+            small_step()
+        run[o[:2]](int(o[2]))
+        seen.append(o[:2])
+        if len(seen) == 2:
+            start_loads(needed[2:])
+            for copy in weight_copies + small_copies:
+                copy.start()
 
     for copy in flight.values():
         copy.wait_recv()
     wait_fifteen(small_all, small_recv.at[1])
     for copy in sent:
         copy.wait_send()
-    for n, buffer in ((0, own_norms), (1, slope_norms.at[0]), (2, slope_norms.at[1])):
+    for n, buffer in [(0, own_norms)] + [(1 + g, slope_norms.at[g]) for g in range(len(GROUPS))]:
         wait_fifteen(buffer, norm_send.at[n])
     wait_fifteen(small_in, small_send.at[0])
     wait_fifteen(small_all, small_send.at[1])
@@ -454,15 +467,15 @@
             pltpu.VMEM((4, 3, 3, HALF, BLOCK), bf16),
             pltpu.VMEM((4, BLOCK, BLOCK), f32),
             pltpu.VMEM((GROUP, 4, BLOCK), f32),
-            pltpu.VMEM((2, GROUP, 2, BLOCK), f32),
+            pltpu.VMEM((len(GROUPS), GROUP, max(map(len, GROUPS)), BLOCK), f32),
             pltpu.VMEM((2, 1, GROUP * BLOCK), f32),
             pltpu.VMEM((GROUP, 2, BLOCK), f32),
             pltpu.VMEM((2, BLOCK), f32),
             pltpu.SemaphoreType.DMA((4, 5)),
-            pltpu.SemaphoreType.DMA((120,)),
-            pltpu.SemaphoreType.DMA((120,)),
-            pltpu.SemaphoreType.DMA((3,)),
-            pltpu.SemaphoreType.DMA((3,)),
+            pltpu.SemaphoreType.DMA((28 * len(CHUNKS),)),
+            pltpu.SemaphoreType.DMA((28 * len(CHUNKS),)),
+            pltpu.SemaphoreType.DMA((1 + len(GROUPS),)),
+            pltpu.SemaphoreType.DMA((1 + len(GROUPS),)),
             pltpu.SemaphoreType.DMA((2,)),
             pltpu.SemaphoreType.DMA((2,)),
             pltpu.SemaphoreType.DMA((4,)),

time: 53.9 us -> 52.5 us (0.974)
  Pallas kernels: 52.8 us -> 51.2 us
    pallas_call x1, Pallas kernels: 51.2 us -> 49.5 us  [per_device(): pl.pallas_call(kernel, out_shape=(pltpu.VMEM((4, *blocks), bf16), pltpu.V...]
where the time goes in v5:
time: 52.5 us; the launch traced here: 51.8 us
  Pallas kernels  51.2 us (98%)
  between operations  0.66 us (1%)
    pallas_call x1, Pallas kernels, per_device(): pl.pallas_call(kernel, out_shape=(pltpu.VMEM((4, *blocks), bf16), pltpu.V...  49.5 us
    pallas_call x1, Pallas kernels, per_device(): pl.pallas_call(write_out, out_shape=(shape(blocks, bf16), shape(blocks, b...  1.68 us

profile of v5, /device:TPU:32, one launch (start us, length us, event | category | flops | bytes accessed | tf_op | source)
XLA Modules:
  0.0 51.8 jit_solution(1193246029436783159)
XLA Ops:
  0.6 49.5 %step.1 = (bf16[4,4,4,128,128]{4,3,2,1,0:T(8,128)(2,1)S(1)}, f32[4,128,128]{2,1,0:T(8,128)S(1)}, f32[16,2,128]{2,1,0:T(2,128)S(1)}, f32[2,128]{1,0:T(2,128)S(1)}) custom-call(f32[4,4,128,128]{3,2,1,0:T(8,128)} %bitcast.13, f32[4,4,128,128]{3,2,1,0:T(8,128)} %bitcast.14, f32[4,4,128,128]{3,2,1,0:T(8,128)} %bitcast.15, f32[128,2048]{1,0:T(8,128)} %bitcast.16, ...), custom_call_target="tpu_custom_call" | custom-call | tf_op jit(solution)/shard_map/step/pallas_call | solution.py:451
  50.2 1.7 %write_out.1 = (bf16[4,4,128,128]{3,2,1,0:T(8,128)(2,1)}, bf16[4,4,128,128]{3,2,1,0:T(8,128)(2,1)}, bf16[4,4,128,128]{3,2,1,0:T(8,128)(2,1)}, bf16[128,2048]{1,0...) custom-call(bf16[4,4,4,128,128]{4,3,2,1,0:T(8,128)(2,1)S(1)} %get-tu, ...), custom_call_target="tpu_custom_call" | custom-call | tf_op jit(solution)/shard_map/write_out/pallas_call | solution.py:494

commit v6 on v5

--- a/solution.py
+++ b/solution.py
@@ -18,10 +18,11 @@
 FIRST = ("x", "y", "x", "y")
 CHUNKS = ((0, 0, 128), (1, 0, 128), (2, 0, 128), (3, 0, 128))
 GROUPS = ((0, 1), (2, 3))
-ORDER = """
-oF1 oF2 oF3 oF0 oN2 oN1 oN3 re2 oN0 re3 re0 re1 cl2 cl3 cl1 cl0 su1 su0 st1 st0 l12 l22 l23 l13
-l10 p00 l21 l11 p23 l20 p22 p03 p01 p13 p12 p02 p10 p21 p11 p20
-""".split()
+ORDER = (
+    "oF0", "oF1", "oF3", "oF2", "oN0", "oN1", "re1", "re0", "oN2", "oN3", "re3", "re2", "cl0", "cl1",
+    "cl2", "cl3", "su0", "su1", "st0", "st1", "l20", "l10", "l21", "l11", "l12", "l23", "l13", "l22",
+    "p03", "p02", "p20", "p21", "p10", "p00", "p11", "p01", "p12", "p23", "p13", "p22",
+)
 FAR_FIRST = (8, 7, 9, 6, 10, 5, 11, 4, 12, 3, 13, 2, 14, 1, 15)
 
 

time: 52.5 us -> 52.2 us (level)
  no operation moved by 1% of the time
where the time goes in v6:
time: 52.2 us; the launch traced here: 51.6 us
  Pallas kernels  50.9 us (98%)
  between operations  0.66 us (1%)
    pallas_call x1, Pallas kernels, per_device(): pl.pallas_call(kernel, out_shape=(pltpu.VMEM((4, *blocks), bf16), pltpu.V...  49.2 us
    pallas_call x1, Pallas kernels, per_device(): pl.pallas_call(write_out, out_shape=(shape(blocks, bf16), shape(blocks, b...  1.68 us

profile of v6, /device:TPU:32, one launch (start us, length us, event | category | flops | bytes accessed | tf_op | source)
XLA Modules:
  0.0 51.6 jit_solution(5875740894859849230)
XLA Ops:
  0.6 49.2 %step.1 = (bf16[4,4,4,128,128]{4,3,2,1,0:T(8,128)(2,1)S(1)}, f32[4,128,128]{2,1,0:T(8,128)S(1)}, f32[16,2,128]{2,1,0:T(2,128)S(1)}, f32[2,128]{1,0:T(2,128)S(1)}) custom-call(f32[4,4,128,128]{3,2,1,0:T(8,128)} %bitcast.13, f32[4,4,128,128]{3,2,1,0:T(8,128)} %bitcast.14, f32[4,4,128,128]{3,2,1,0:T(8,128)} %bitcast.15, f32[128,2048]{1,0:T(8,128)} %bitcast.16, ...), custom_call_target="tpu_custom_call" | custom-call | tf_op jit(solution)/shard_map/step/pallas_call | solution.py:452
  49.9 1.7 %write_out.1 = (bf16[4,4,128,128]{3,2,1,0:T(8,128)(2,1)}, bf16[4,4,128,128]{3,2,1,0:T(8,128)(2,1)}, bf16[4,4,128,128]{3,2,1,0:T(8,128)(2,1)}, bf16[128,2048]{1,0...) custom-call(bf16[4,4,4,128,128]{4,3,2,1,0:T(8,128)(2,1)S(1)} %get-tu, ...), custom_call_target="tpu_custom_call" | custom-call | tf_op jit(solution)/shard_map/write_out/pallas_call | solution.py:495

commit v7 on v6

--- a/solution.py
+++ b/solution.py
@@ -19,9 +19,9 @@
 CHUNKS = ((0, 0, 128), (1, 0, 128), (2, 0, 128), (3, 0, 128))
 GROUPS = ((0, 1), (2, 3))
 ORDER = (
-    "oF0", "oF1", "oF3", "oF2", "oN0", "oN1", "re1", "re0", "oN2", "oN3", "re3", "re2", "cl0", "cl1",
-    "cl2", "cl3", "su0", "su1", "st0", "st1", "l20", "l10", "l21", "l11", "l12", "l23", "l13", "l22",
-    "p03", "p02", "p20", "p21", "p10", "p00", "p11", "p01", "p12", "p23", "p13", "p22",
+    "oF0", "oF1", "oF2", "oN0", "oF3", "oN1", "re0", "re1", "oN3", "re2", "oN2", "re3", "cl1", "cl0",
+    "cl2", "cl3", "su0", "su1", "st0", "st1", "l10", "l11", "l21", "l20", "l22", "l12", "l23", "l13",
+    "p10", "p21", "p03", "p11", "p20", "p22", "p02", "p23", "p00", "p01", "p12", "p13",
 )
 FAR_FIRST = (8, 7, 9, 6, 10, 5, 11, 4, 12, 3, 13, 2, 14, 1, 15)
 
@@ -48,7 +48,7 @@
 
 FIRST_STEPS = 118 * 256.0
 SECOND_STEPS = 127 * 256.0
-SLAB = 32
+SLAB = 64
 
 
 def rounded(a):

time: 52.2 us -> 51.7 us (level)
  no operation moved by 1% of the time
where the time goes in v7:
time: 51.7 us; the launch traced here: 51.2 us
  Pallas kernels  50.5 us (98%)
  between operations  0.66 us (1%)
    pallas_call x1, Pallas kernels, per_device(): pl.pallas_call(kernel, out_shape=(pltpu.VMEM((4, *blocks), bf16), pltpu.V...  48.8 us
    pallas_call x1, Pallas kernels, per_device(): pl.pallas_call(write_out, out_shape=(shape(blocks, bf16), shape(blocks, b...  1.68 us

profile of v7, /device:TPU:32, one launch (start us, length us, event | category | flops | bytes accessed | tf_op | source)
XLA Modules:
  0.0 51.2 jit_solution(13145612634544242984)
XLA Ops:
  0.6 48.8 %step.1 = (bf16[4,4,4,128,128]{4,3,2,1,0:T(8,128)(2,1)S(1)}, f32[4,128,128]{2,1,0:T(8,128)S(1)}, f32[16,2,128]{2,1,0:T(2,128)S(1)}, f32[2,128]{1,0:T(2,128)S(1)}) custom-call(f32[4,4,128,128]{3,2,1,0:T(8,128)} %bitcast.13, f32[4,4,128,128]{3,2,1,0:T(8,128)} %bitcast.14, f32[4,4,128,128]{3,2,1,0:T(8,128)} %bitcast.15, f32[128,2048]{1,0:T(8,128)} %bitcast.16, ...), custom_call_target="tpu_custom_call" | custom-call | tf_op jit(solution)/shard_map/step/pallas_call | solution.py:452
  49.5 1.7 %write_out.1 = (bf16[4,4,128,128]{3,2,1,0:T(8,128)(2,1)}, bf16[4,4,128,128]{3,2,1,0:T(8,128)(2,1)}, bf16[4,4,128,128]{3,2,1,0:T(8,128)(2,1)}, bf16[128,2048]{1,0...) custom-call(bf16[4,4,4,128,128]{4,3,2,1,0:T(8,128)(2,1)S(1)} %get-tu, ...), custom_call_target="tpu_custom_call" | custom-call | tf_op jit(solution)/shard_map/write_out/pallas_call | solution.py:495

commit v8 on v7

--- a/solution.py
+++ b/solution.py
@@ -172,7 +172,7 @@
             body(pl.multiple_of(start + i * SLAB, SLAB))
             return carry
 
-        lax.fori_loop(0, count // SLAB, one, 0)
+        lax.fori_loop(0, count // SLAB, one, 0, unroll=True)
 
     def cut(r):
         return pl.ds(r, SLAB)

time: 51.7 us -> 51.7 us (level)
  no operation moved by 1% of the time
where the time goes in v8:
time: 51.7 us; the launch traced here: 51.1 us
  Pallas kernels  50.5 us (98%)
  between operations  0.66 us (1%)
    pallas_call x1, Pallas kernels, per_device(): pl.pallas_call(kernel, out_shape=(pltpu.VMEM((4, *blocks), bf16), pltpu.V...  48.8 us
    pallas_call x1, Pallas kernels, per_device(): pl.pallas_call(write_out, out_shape=(shape(blocks, bf16), shape(blocks, b...  1.68 us

profile of v8, /device:TPU:32, one launch (start us, length us, event | category | flops | bytes accessed | tf_op | source)
XLA Modules:
  0.0 51.1 jit_solution(9516474714778495102)
XLA Ops:
  0.6 48.8 %step.1 = (bf16[4,4,4,128,128]{4,3,2,1,0:T(8,128)(2,1)S(1)}, f32[4,128,128]{2,1,0:T(8,128)S(1)}, f32[16,2,128]{2,1,0:T(2,128)S(1)}, f32[2,128]{1,0:T(2,128)S(1)}) custom-call(f32[4,4,128,128]{3,2,1,0:T(8,128)} %bitcast.13, f32[4,4,128,128]{3,2,1,0:T(8,128)} %bitcast.14, f32[4,4,128,128]{3,2,1,0:T(8,128)} %bitcast.15, f32[128,2048]{1,0:T(8,128)} %bitcast.16, ...), custom_call_target="tpu_custom_call" | custom-call | tf_op jit(solution)/shard_map/step/pallas_call | solution.py:452
  49.4 1.7 %write_out.1 = (bf16[4,4,128,128]{3,2,1,0:T(8,128)(2,1)}, bf16[4,4,128,128]{3,2,1,0:T(8,128)(2,1)}, bf16[4,4,128,128]{3,2,1,0:T(8,128)(2,1)}, bf16[128,2048]{1,0...) custom-call(bf16[4,4,4,128,128]{4,3,2,1,0:T(8,128)(2,1)S(1)} %get-tu, ...), custom_call_target="tpu_custom_call" | custom-call | tf_op jit(solution)/shard_map/write_out/pallas_call | solution.py:495
